TPU v7x, 1024 devices: a whole 4x8x16 slice. The times are simulated.
1024 devices in a mesh: gx: 16 (over y, core), gy: 8 (over x, z_hi), gz: 8 (over z_lo).
Axes of the slice: x: 4, y: 8, z: 16 (z_hi: 2, z_lo: 8; z = z_hi * 8 + z_lo), core: 2. Of those that a mesh axis runs over, the one named last changes fastest.
Arguments:
- density: float32 [128, 128, 1024], P('gx', 'gy', 'gz'), may hold values from 0.7 to 1.6
- momentum: float32 [128, 128, 1024], P('gx', 'gy', 'gz'), may hold values from -7 to 7
- hydrogen: float32 [128, 128, 1024], P('gx', 'gy', 'gz'), may hold values from 0.05 to 1.2
- forced_modes: int32 [96, 3], replicated, may hold values from -3 to 3, as said below
Outputs:
- density_rate: float32 [128, 128, 1024], P('gx', 'gy', 'gz')
- momentum_rate: float32 [128, 128, 1024], P('gx', 'gy', 'gz')
- hydrogen_rate: float32 [128, 128, 1024], P('gx', 'gy', 'gz')
Inputs may be any that keep to these rules, and one draw needn't show every extreme that they name: `forced_modes`: each row is a wave vector (kx, ky, kz) with 1 <= kx^2 + ky^2 + kz^2 <= 9; the 96 rows are distinct.
All inputs are finite; a program needn't handle non-finite values.
Results may differ from a plain program's by a relative error of at most 0.0003.
Values sent between devices are 32-bit elements; how exact they have to be, the bound alone decides.
No kernel may reach another device: no remote copies, remote signals or barrier semaphores. Data moves between devices by JAX's collectives and lax.ppermute only.
A program may use at most 32 MiB of HBM per device.

v0:
```python
import jax
import jax.numpy as jnp
from jax import lax
from jax.sharding import Mesh
from jax.sharding import PartitionSpec as P

KMAX = 3
GX = ("gx_0", "gx_1")
GY = ("gy_0", "gy_1")
GX_GY_GZ = ("gx_0", "gx_1", "gy_0", "gy_1", "gz")


FIRST_COEFFS = (0.8, -0.2, 4.0 / 105.0, -1.0 / 280.0)
SECOND_COEFFS = (1.6, -0.2, 8.0 / 315.0, -1.0 / 560.0)
CENTRE_COEFF = -205.0 / 72.0
VISCOSITY = 0.3
DIFFUSIVITY = 1.5
FORCE_POWER = 0.3
ENERGY_EPS = 1e-06
ACTIVATION = 2.0
HIGHEST = lax.Precision.HIGHEST


def over_axes(x, axes):
    for axis in axes:
        x = lax.psum(x, axis)
    return x


def padded_2(x, sides, width):
    for axis, dim in sides:
        size, length = (lax.axis_size(axis), x.shape[dim])
        up = [(i, (i + 1) % size) for i in range(size)]
        down = [(j, i) for i, j in up]
        last = lax.slice_in_dim(x, length - width, length, axis=dim)
        first = lax.slice_in_dim(x, 0, width, axis=dim)
        before = lax.ppermute(last, axis, up)
        after = lax.ppermute(first, axis, down)
        x = jnp.concatenate([before, x, after], axis=dim)
    return x


def shifted(padded, axis, offset, length):
    return lax.slice_in_dim(padded, 4 + offset, 4 + offset + length, axis=axis)


def first_diff(padded, axis, length):
    total = jnp.zeros_like(shifted(padded, axis, 0, length))
    for offset, weight in enumerate(FIRST_COEFFS, 1):
        total = total + weight * (
            shifted(padded, axis, offset, length) - shifted(padded, axis, -offset, length)
        )
    return total


def second_diff(padded, axis, length):
    total = CENTRE_COEFF * shifted(padded, axis, 0, length)
    for offset, weight in enumerate(SECOND_COEFFS, 1):
        total = total + weight * (
            shifted(padded, axis, offset, length) + shifted(padded, axis, -offset, length)
        )
    return total


def wave_tables(start, local, total):
    position = start + jnp.arange(local, dtype=jnp.int32)
    wavenum = jnp.arange(-KMAX, KMAX + 1, dtype=jnp.int32)
    phase = wavenum[:, None] * position[None, :] % total
    angle = 2.0 * jnp.pi / total * phase.astype(jnp.float32)
    return (jnp.cos(angle), jnp.sin(angle))


def modal_force(velocity, forced_modes):
    size_x, size_y, size_z = velocity.shape
    full_x = size_x * lax.axis_size(GX)
    full_y = size_y * lax.axis_size(GY)
    full_z = size_z * lax.axis_size("gz")
    cos_x, sin_x = wave_tables(lax.axis_index(GX) * size_x, size_x, full_x)
    cos_y, sin_y = wave_tables(lax.axis_index(GY) * size_y, size_y, full_y)
    cos_z, sin_z = wave_tables(lax.axis_index("gz") * size_z, size_z, full_z)
    flat = velocity.reshape(size_x * size_y, size_z)
    contract = (((1,), (1,)), ((), ()))
    part_re = lax.dot_general(cos_z, flat, contract, precision=HIGHEST).reshape(-1, size_x, size_y)
    part_im = lax.dot_general(sin_z, flat, contract, precision=HIGHEST).reshape(-1, size_x, size_y)
    mid_re = jnp.einsum("axy,by->abx", part_re, cos_y, precision=HIGHEST) - jnp.einsum(
        "axy,by->abx", part_im, sin_y, precision=HIGHEST
    )
    mid_im = jnp.einsum("axy,by->abx", part_re, sin_y, precision=HIGHEST) + jnp.einsum(
        "axy,by->abx", part_im, cos_y, precision=HIGHEST
    )
    cube_re = jnp.einsum("abx,cx->cba", mid_re, cos_x, precision=HIGHEST) - jnp.einsum(
        "abx,cx->cba", mid_im, sin_x, precision=HIGHEST
    )
    cube_im = jnp.einsum("abx,cx->cba", mid_re, sin_x, precision=HIGHEST) + jnp.einsum(
        "abx,cx->cba", mid_im, cos_x, precision=HIGHEST
    )
    width = 2 * KMAX + 1
    code = (
        (forced_modes[:, 0] + KMAX) * width * width
        + (forced_modes[:, 1] + KMAX) * width
        + (forced_modes[:, 2] + KMAX)
    )
    selector = (code[:, None] == jnp.arange(width**3, dtype=jnp.int32)[None, :]).astype(jnp.float32)
    local_cos = jnp.dot(selector, cube_re.reshape(-1), precision=HIGHEST)
    local_sin = jnp.dot(selector, cube_im.reshape(-1), precision=HIGHEST)
    summed = (over_axes(local_cos, GX_GY_GZ), over_axes(local_sin, GX_GY_GZ))
    ncell = float(full_x * full_y * full_z)
    coef_cos = summed[0] / ncell
    coef_sin = summed[1] / ncell
    energy = jnp.sum(coef_cos * coef_cos + coef_sin * coef_sin)
    spec_re = jnp.dot(selector.T, coef_cos, precision=HIGHEST).reshape(width, width, width)
    spec_im = -jnp.dot(selector.T, coef_sin, precision=HIGHEST).reshape(width, width, width)
    step_re = jnp.einsum("abc,ax->xbc", spec_re, cos_x, precision=HIGHEST) - jnp.einsum(
        "abc,ax->xbc", spec_im, sin_x, precision=HIGHEST
    )
    step_im = jnp.einsum("abc,ax->xbc", spec_re, sin_x, precision=HIGHEST) + jnp.einsum(
        "abc,ax->xbc", spec_im, cos_x, precision=HIGHEST
    )
    plane_re = jnp.einsum("xbc,by->xyc", step_re, cos_y, precision=HIGHEST) - jnp.einsum(
        "xbc,by->xyc", step_im, sin_y, precision=HIGHEST
    )
    plane_im = jnp.einsum("xbc,by->xyc", step_re, sin_y, precision=HIGHEST) + jnp.einsum(
        "xbc,by->xyc", step_im, cos_y, precision=HIGHEST
    )
    low = 2.0 * (
        jnp.dot(plane_re.reshape(-1, width), cos_z, precision=HIGHEST)
        - jnp.dot(plane_im.reshape(-1, width), sin_z, precision=HIGHEST)
    )
    return FORCE_POWER * low.reshape(size_x, size_y, size_z) / (energy + ENERGY_EPS)


def stencil_terms(density, momentum, hydrogen):
    size_x, size_y, size_z = density.shape
    fields = jnp.stack([density, momentum, hydrogen])
    stream_pad = padded_2(fields, ((GX, 1),), 4)
    dens_pad = stream_pad[0]
    mom_pad = stream_pad[1]
    fuel_pad = stream_pad[2]
    vel_pad = mom_pad / dens_pad
    velocity = momentum / density
    mass_div = first_diff(mom_pad, 0, size_x)
    mom_div = first_diff(mom_pad * vel_pad + dens_pad, 0, size_x)
    fuel_div = first_diff(fuel_pad * vel_pad, 0, size_x)
    diffused = second_diff(stream_pad[1:], 1, size_x)
    carried = fields[1:]
    span_pad = padded_2(carried, ((GY, 2), ("gz", 3)), 4)
    side_pad = span_pad[:, :, :, 4 : 4 + size_z]
    depth_pad = span_pad[:, :, 4 : 4 + size_y, :]
    diffused = diffused + second_diff(side_pad, 2, size_y) + second_diff(depth_pad, 3, size_z)
    density_rate = -mass_div
    momentum_part = -mom_div + VISCOSITY * diffused[0]
    hydrogen_rate = (
        -fuel_div + DIFFUSIVITY * diffused[1] - hydrogen * jnp.exp(-ACTIVATION * hydrogen / density)
    )
    return (density_rate, momentum_part, hydrogen_rate, velocity)


def per_device(density, momentum, hydrogen, forced_modes):
    density_rate, momentum_part, hydrogen_rate, velocity = stencil_terms(
        density, momentum, hydrogen
    )
    force = modal_force(velocity, forced_modes)
    momentum_rate = momentum_part + density * force
    return (density_rate, momentum_rate, hydrogen_rate)


def solution(mesh):
    split = Mesh(
        mesh.devices.reshape(8, 2, 4, 2, mesh.shape["gz"]), ("gx_0", "gx_1", "gy_0", "gy_1", "gz")
    )
    in_specs = (P(GX, GY, "gz"), P(GX, GY, "gz"), P(GX, GY, "gz"), P())
    out_specs = (P(GX, GY, "gz"), P(GX, GY, "gz"), P(GX, GY, "gz"))
    return jax.shard_map(
        per_device, mesh=split, in_specs=in_specs, out_specs=out_specs, check_vma=False
    )
```

profile of v0, /device:TPU:8, one launch (start us, length us, event | category | flops | bytes accessed | tf_op | source)
XLA Modules:
  0.0 132.5 jit_solution(6043404160377474992)
XLA Ops:
  0.7 0.9 fusion.73
  1.5 21.6 %collective-permute-start.2 = (f32[2,8,4,128]{3,2,1,0:T(4,128)S(1)}, f32[2,8,4,128]{3,2,1,0:T(4,128)S(1)}, u32[]{:S(2)}, u32[]{:S(2)}) collective-permute-start(f32[2,8,4,128]{3,2,1,0:T(4,128)S(1)} %get-tuple-element.26), channel_id=1, source_target_pairs={{8,0},{16,8},{24,16},{32,24},{40,32},{48,40},{56,48},{0,56},{9,1},... | collective-permute-start | bytes 98312 | tf_op jit(solution)/shard_map/ppermute | solution.py:38
  23.1 1.9 %collective-permute-start.3 = (f32[2,8,4,128]{3,2,1,0:T(4,128)S(1)}, f32[2,8,4,128]{3,2,1,0:T(4,128)S(1)}, u32[]{:S(2)}, u32[]{:S(2)}) collective-permute-start(f32[2,8,4,128]{3,2,1,0:T(4,128)S(1)} %get-tuple-element.25), channel_id=1, source_target_pairs={{0,8},{8,16},{16,24},{24,32},{32,40},{40,48},{48,56},{56,0},{1,9},... | collective-permute-start | bytes 98312 | tf_op jit(solution)/shard_map/ppermute | solution.py:37
  25.1 0.5 collective-permute-start.1
  25.6 0.6 fusion.107
  26.3 0.7 fusion.100
  26.9 0.5 fusion.84
  27.5 0.5 fusion.82
  28.0 0.5 fusion.7
  28.5 0.6 fusion.95
  29.1 0.6 fusion.110
  29.7 0.6 fusion.6
  30.3 0.6 fusion.4
  31.2 0.6 copy-done.3
  31.7 0.6 fusion.5
  33.1 18.3 %all-reduce.1 = (f32[96]{0:T(128)S(1)}, f32[96]{0:T(128)S(1)}) all-reduce(f32[96]{0:T(128)S(1)} %convolution_bitcast_fusion.1, f32[96]{0:T(128)S(1)} %convolution_bitcast_fusion), channel_id=1, replica_groups=mesh['gx_0'=8,'gx_1'=2,'gy_0'=4,'gy_1'=2,'gz'=8] {'gx_0'}, use_global_device_ids=true, to_apply=%region_0.1 | all-reduce | flops 192 | bytes 1536 | tf_op jit(solution)/shard_map/psum | solution.py:26
  51.4 2.5 %all-reduce.4 = (f32[96]{0:T(128)S(1)}, f32[96]{0:T(128)S(1)}) all-reduce(f32[96]{0:T(128)S(1)} %get-tuple-element.5, f32[96]{0:T(128)S(1)} %get-tuple-element.6), channel_id=1, replica_groups=mesh['gx_0'=8,'gx_1'=2,'gy_0'=4,'gy_1'=2,'gz'=8] {'gx_1'}, use_global_device_ids=true, to_apply=%region_1.2 | all-reduce | flops 192 | bytes 1536 | tf_op jit(solution)/shard_map/psum | solution.py:26
  53.9 7.7 %all-reduce.2 = (f32[96]{0:T(128)S(1)}, f32[96]{0:T(128)S(1)}) all-reduce(f32[96]{0:T(128)S(1)} %get-tuple-element.11, f32[96]{0:T(128)S(1)} %get-tuple-element.12), channel_id=1, replica_groups=mesh['gx_0'=8,'gx_1'=2,'gy_0'=4,'gy_1'=2,'gz'=8] {'gy_0'}, use_global_device_ids=true, to_apply=%region_2.3 | all-reduce | flops 192 | bytes 1536 | tf_op jit(solution)/shard_map/psum | solution.py:26
  61.6 14.4 %all-reduce.3 = (f32[96]{0:T(128)S(1)}, f32[96]{0:T(128)S(1)}) all-reduce(f32[96]{0:T(128)S(1)} %get-tuple-element.7, f32[96]{0:T(128)S(1)} %get-tuple-element.8), channel_id=1, replica_groups=mesh['gx_0'=8,'gx_1'=2,'gy_0'=4,'gy_1'=2,'gz'=8] {'gy_1'}, use_global_device_ids=true, to_apply=%region_3.4 | all-reduce | flops 192 | bytes 1536 | tf_op jit(solution)/shard_map/psum | solution.py:26
  76.0 32.0 %all-reduce = (f32[96]{0:T(128)S(1)}, f32[96]{0:T(128)S(1)}) all-reduce(f32[96]{0:T(128)S(1)} %get-tuple-element.9, f32[96]{0:T(128)S(1)} %get-tuple-element.10), channel_id=1, replica_groups=mesh['gx_0'=8,'gx_1'=2,'gy_0'=4,'gy_1'=2,'gz'=8] {'gz'}, use_global_device_ids=true, to_apply=%region_4.5 | all-reduce | flops 192 | bytes 1536 | tf_op jit(solution)/shard_map/psum | solution.py:26
  108.3 0.6 add_reduce_fusion
  111.8 0.3 fusion.3
  112.1 0.3 fusion.121
  113.1 0.3 fusion.1
  113.6 1.9 %collective-permute-start.4 = (f32[2,8,24,4]{3,2,1,0:T(8,128)S(1)}, f32[2,8,24,4]{3,2,1,0:T(8,128)S(1)}, u32[]{:S(2)}, u32[]{:S(2)}) collective-permute-start(f32[2,8,24,4]{3,2,1,0:T(8,128)S(1)} %get-tuple-element.17), channel_id=1, source_target_pairs={{1,0},{2,1},{3,2},{4,3},{5,4},{6,5},{7,6},{0,7},{9,8},{10,9},{11,1... | collective-permute-start | bytes 18440 | tf_op jit(solution)/shard_map/ppermute | solution.py:38
  115.6 3.9 %collective-permute-start.5 = (f32[2,8,24,4]{3,2,1,0:T(8,128)S(1)}, f32[2,8,24,4]{3,2,1,0:T(8,128)S(1)}, u32[]{:S(2)}, u32[]{:S(2)}) collective-permute-start(f32[2,8,24,4]{3,2,1,0:T(8,128)S(1)} %get-tuple-element.18), channel_id=1, source_target_pairs={{0,1},{1,2},{2,3},{3,4},{4,5},{5,6},{6,7},{7,0},{8,9},{9,10},{10,1... | collective-permute-start | bytes 18440 | tf_op jit(solution)/shard_map/ppermute | solution.py:37
  119.5 3.8 %collective-permute-done.4 = f32[2,8,24,4]{3,2,1,0:T(8,128)S(1)} collective-permute-done((f32[2,8,24,4]{3,2,1,0:T(8,128)S(1)}, f32[2,8,24,4]{3,2,1,0:T(8,128)S(1)}, u32[]{:S(2)}, u32[]{:S(2)}) %collective-permute-start.4) | collective-permute-done | bytes 6176 | tf_op jit(solution)/shard_map/ppermute | solution.py:38
  123.3 6.4 %collective-permute-done.5 = f32[2,8,24,4]{3,2,1,0:T(8,128)S(1)} collective-permute-done((f32[2,8,24,4]{3,2,1,0:T(8,128)S(1)}, f32[2,8,24,4]{3,2,1,0:T(8,128)S(1)}, u32[]{:S(2)}, u32[]{:S(2)}) %collective-permute-start.5) | collective-permute-done | bytes 6176 | tf_op jit(solution)/shard_map/ppermute | solution.py:37
  130.1 0.7 fusion.66
  130.8 0.3 fusion.12
  131.1 0.7 fusion.43
  131.8 0.7 fusion.54
  (48 shorter events, 4.8 us)
Async XLA Ops:
  0.6 24.4 %copy-start = (f32[8,16,128]{2,1,0:T(8,128)S(1)}, f32[8,16,128]{2,1,0:T(8,128)}, u32[]{:S(2)}) copy-start(f32[8,16,128]{2,1,0:T(8,128)} %param.6) | copy-start | bytes 196612
  0.6 24.4 %copy-start.1 = (f32[8,16,128]{2,1,0:T(8,128)S(1)}, f32[8,16,128]{2,1,0:T(8,128)}, u32[]{:S(2)}) copy-start(f32[8,16,128]{2,1,0:T(8,128)} %param.5) | copy-start | bytes 196612
  0.7 24.4 %copy-start.2 = (f32[8,16,128]{2,1,0:T(8,128)S(1)}, f32[8,16,128]{2,1,0:T(8,128)}, u32[]{:S(2)}) copy-start(f32[8,16,128]{2,1,0:T(8,128)} %param.4) | copy-start | bytes 196612
  1.5 111.9 %collective-permute-start.2 = (f32[2,8,4,128]{3,2,1,0:T(4,128)S(1)}, f32[2,8,4,128]{3,2,1,0:T(4,128)S(1)}, u32[]{:S(2)}, u32[]{:S(2)}) collective-permute-start(f32[2,8,4,128]{3,2,1,0:T(4,128)S(1)} %get-tuple-element.26), channel_id=1, source_target_pairs={{8,0},{16,8},{24,16},{32,24},{40,32},{48,40},{56,48},{0,56},{9,1},... | collective-permute-start | bytes 98312 | tf_op jit(solution)/shard_map/ppermute | solution.py:38
  23.1 90.4 %collective-permute-start.3 = (f32[2,8,4,128]{3,2,1,0:T(4,128)S(1)}, f32[2,8,4,128]{3,2,1,0:T(4,128)S(1)}, u32[]{:S(2)}, u32[]{:S(2)}) collective-permute-start(f32[2,8,4,128]{3,2,1,0:T(4,128)S(1)} %get-tuple-element.25), channel_id=1, source_target_pairs={{0,8},{8,16},{16,24},{24,32},{32,40},{40,48},{48,56},{56,0},{1,9},... | collective-permute-start | bytes 98312 | tf_op jit(solution)/shard_map/ppermute | solution.py:37
  25.1 104.9 %collective-permute-start = (f32[3,4,16,128]{3,2,1,0:T(8,128)S(1)}, f32[3,4,16,128]{3,2,1,0:T(8,128)S(1)}, u32[]{:S(2)}, u32[]{:S(2)}) collective-permute-start(f32[3,4,16,128]{3,2,1,0:T(8,128)S(1)} %get-tuple-element.21), channel_id=1, source_target_pairs={{64,0},{128,64},{192,128},{256,192},{320,256},{384,320},{448,384},... | collective-permute-start | bytes 294920 | tf_op jit(solution)/shard_map/ppermute | solution.py:38
  25.1 104.9 %collective-permute-start.1 = (f32[3,4,16,128]{3,2,1,0:T(8,128)S(1)}, f32[3,4,16,128]{3,2,1,0:T(8,128)S(1)}, u32[]{:S(2)}, u32[]{:S(2)}) collective-permute-start(f32[3,4,16,128]{3,2,1,0:T(8,128)S(1)} %get-tuple-element.22), channel_id=1, source_target_pairs={{0,64},{64,128},{128,192},{192,256},{256,320},{320,384},{384,448},... | collective-permute-start | bytes 294920 | tf_op jit(solution)/shard_map/ppermute | solution.py:37
  31.0 0.7 copy-start.3
  113.6 9.7 %collective-permute-start.4 = (f32[2,8,24,4]{3,2,1,0:T(8,128)S(1)}, f32[2,8,24,4]{3,2,1,0:T(8,128)S(1)}, u32[]{:S(2)}, u32[]{:S(2)}) collective-permute-start(f32[2,8,24,4]{3,2,1,0:T(8,128)S(1)} %get-tuple-element.17), channel_id=1, source_target_pairs={{1,0},{2,1},{3,2},{4,3},{5,4},{6,5},{7,6},{0,7},{9,8},{10,9},{11,1... | collective-permute-start | bytes 18440 | tf_op jit(solution)/shard_map/ppermute | solution.py:38
  115.6 14.2 %collective-permute-start.5 = (f32[2,8,24,4]{3,2,1,0:T(8,128)S(1)}, f32[2,8,24,4]{3,2,1,0:T(8,128)S(1)}, u32[]{:S(2)}, u32[]{:S(2)}) collective-permute-start(f32[2,8,24,4]{3,2,1,0:T(8,128)S(1)} %get-tuple-element.18), channel_id=1, source_target_pairs={{0,1},{1,2},{2,3},{3,4},{4,5},{5,6},{6,7},{7,0},{8,9},{9,10},{10,1... | collective-permute-start | bytes 18440 | tf_op jit(solution)/shard_map/ppermute | solution.py:37
where the time goes:
time: 133 us
  blocking collectives  75 us (56%)
  starting transfers between devices  29.8 us (22%)
  waiting for transfers between devices  10.2 us (8%)
  matrix products  9.66 us (7%)
  other arithmetic  4.3 us (3%)
  local copies, waits for them, and re-layouts  1.92 us (1%)
  between operations  1.63 us (1%)
    psum x5, blocking collectives, over_axes(): x = lax.psum(x, axis)  75 us
    ppermute x3, starting transfers between devices, padded_2(): after = lax.ppermute(first, axis, down)  23.5 us
    ppermute x3, waiting for transfers between devices, padded_2(): before = lax.ppermute(last, axis, up)  6.43 us
    ppermute x3, starting transfers between devices, padded_2(): before = lax.ppermute(last, axis, up)  6.34 us
    ppermute x3, waiting for transfers between devices, padded_2(): after = lax.ppermute(first, axis, down)  3.78 us
  transfers between devices with their start and end apart: 6, of which 2 were waited for; matrix products, arithmetic and copies ran while one was open for 9% of the time, Pallas kernels for 0%

commit v1 on v0

v1 whole, which is shorter than its diff:
```python
import functools

import jax
import jax.numpy as jnp
from jax import lax
from jax.experimental import pallas as pl
from jax.experimental.pallas import tpu as pltpu
from jax.sharding import Mesh
from jax.sharding import PartitionSpec as P

GX = ("gx_0", "gx_1")
GY = ("gy_0", "gy_1")
GZ = ("gz",)
FIRST_GROUP = ("gx_0", "gy_0")
SECOND_GROUP = ("gx_1", "gy_1", "gz")

FIRST_COEFFS = (0.8, -0.2, 4.0 / 105.0, -1.0 / 280.0)
SECOND_COEFFS = (1.6, -0.2, 8.0 / 315.0, -1.0 / 560.0)
CENTRE_COEFF = -205.0 / 72.0
VISCOSITY = 0.3
DIFFUSIVITY = 1.5
FORCE_POWER = 0.3
ENERGY_EPS = 1e-06
ACTIVATION = 2.0
HIGHEST = lax.Precision.HIGHEST
LANES = 128
VMEM = pl.BlockSpec(memory_space=pltpu.VMEM)


def row_of(column):
    count = column.shape[0]
    row = lax.broadcasted_iota(jnp.int32, (count, LANES), 0)
    lane = lax.broadcasted_iota(jnp.int32, (count, LANES), 1)
    spread = jnp.broadcast_to(column, (count, LANES))
    return jnp.sum(jnp.where(row == lane, spread, 0.0), axis=0, keepdims=True)


def angles(wave, start, step, count, total):
    index = lax.broadcasted_iota(jnp.int32, (count, LANES), 0)
    position = (start + step * index).astype(jnp.float32)
    phase = wave * position
    phase = phase - total * jnp.round(phase * (1.0 / total))
    return (2.0 * jnp.pi / total) * phase


def partial_kernel(
    full, copies, dens_ref, mom_ref, fuel_ref, modes_ref,
    part_ref, cos_ref, sin_ref, depth_ref,
    xlo_ref, xhi_ref, ylo_ref, yhi_ref, zlo_ref, zhi_ref,
):
    size_x, size_y, size_z = mom_ref.shape
    rows = size_x * size_y
    half = 4
    for n, ref in enumerate((dens_ref, mom_ref, fuel_ref)):
        xlo_ref[n] = ref[0:half]
        xhi_ref[n] = ref[size_x - half : size_x]
    for n, ref in enumerate((mom_ref, fuel_ref)):
        ylo_ref[n] = ref[:, 0:half, :]
        yhi_ref[n] = ref[:, size_y - half : size_y, :]
    turned = [ref[...].reshape(rows, size_z).T for ref in (mom_ref, fuel_ref)]
    zlo_ref[...] = jnp.concatenate([t[0:half] for t in turned], axis=0)
    zhi_ref[...] = jnp.concatenate([t[size_z - half : size_z] for t in turned], axis=0)
    modes = modes_ref[...].astype(jnp.float32)
    wave_x, wave_y, wave_z = (row_of(modes[:, n : n + 1]) for n in range(3))
    base_x = (lax.axis_index("gx_0") * 2 + lax.axis_index("gx_1")) * size_x
    base_y = (lax.axis_index("gy_0") * 2 + lax.axis_index("gy_1")) * size_y
    base_z = lax.axis_index("gz") * size_z
    fine = size_z // 8
    angle = jnp.concatenate(
        [
            angles(wave_x, base_x, 1, size_x, full[0]),
            angles(wave_y, base_y, 1, size_y, full[1]),
            angles(wave_z, base_z, fine, 8, full[2]),
            angles(wave_z, 0, 1, fine, full[2]),
        ],
        axis=0,
    )
    cos, sin = jnp.cos(angle), jnp.sin(angle)
    at_y, at_z, at_f = size_x, size_x + size_y, size_x + size_y + 8
    cy, sy = cos[at_y:at_z], sin[at_y:at_z]
    live = lax.broadcasted_iota(jnp.int32, (1, LANES), 1) < modes_ref.shape[0]
    cf = jnp.where(live, cos[at_f:], 0.0)
    sf = jnp.where(live, sin[at_f:], 0.0)
    for n in range(size_x):
        cx, sx = cos[n : n + 1], sin[n : n + 1]
        cos_ref[n] = cx * cy - sx * sy
        sin_ref[n] = sx * cy + cx * sy
    for n in range(8):
        cz, sz = cos[at_z + n : at_z + n + 1], sin[at_z + n : at_z + n + 1]
        depth_ref[n * fine : (n + 1) * fine, 0:LANES] = cz * cf - sz * sf
        depth_ref[n * fine : (n + 1) * fine, LANES:] = sz * cf + cz * sf
    velocity = (mom_ref[...] / dens_ref[...]).reshape(rows, size_z)
    along = jnp.dot(velocity, depth_ref[...], precision=HIGHEST, preferred_element_type=jnp.float32)
    real, imag = along[:, 0:LANES], along[:, LANES:]
    cos_xy = cos_ref[...].reshape(rows, LANES)
    sin_xy = sin_ref[...].reshape(rows, LANES)
    part_cos = jnp.sum(cos_xy * real - sin_xy * imag, axis=0, keepdims=True)
    part_sin = jnp.sum(sin_xy * real + cos_xy * imag, axis=0, keepdims=True)
    both = jnp.concatenate([part_cos, part_sin], axis=0)
    part_ref[...] = jnp.broadcast_to(both[None], (copies, 2, LANES))


def partial_sums(density, momentum, hydrogen, modes, full, copies):
    size_x, size_y, size_z = density.shape
    f32 = jnp.float32
    shapes = (
        (copies, 2, LANES),
        (size_x, size_y, LANES),
        (size_x, size_y, LANES),
        (size_z, 2 * LANES),
        (3, 4, size_y, size_z),
        (3, 4, size_y, size_z),
        (2, size_x, 4, size_z),
        (2, size_x, 4, size_z),
        (8, size_x * size_y),
        (8, size_x * size_y),
    )
    return pl.pallas_call(
        functools.partial(partial_kernel, full, copies),
        out_shape=[jax.ShapeDtypeStruct(s, f32) for s in shapes],
        in_specs=[VMEM] * 4,
        out_specs=[VMEM] * len(shapes),
        compiler_params=pltpu.CompilerParams(vmem_limit_bytes=16 << 20),
        name="partial_sums",
    )(density, momentum, hydrogen, modes)


def first_diff(planes, at):
    total = None
    for offset, weight in enumerate(FIRST_COEFFS, 1):
        term = weight * (planes[at + offset] - planes[at - offset])
        total = term if total is None else total + term
    return total


def second_diff(pick):
    total = CENTRE_COEFF * pick(0)
    for offset, weight in enumerate(SECOND_COEFFS, 1):
        total = total + weight * (pick(offset) + pick(-offset))
    return total


def final_kernel(
    ncell, dens_ref, mom_ref, fuel_ref, summed_ref, cos_ref, sin_ref, depth_ref,
    xbefore_ref, xafter_ref, ybefore_ref, yafter_ref, zbefore_ref, zafter_ref,
    dens_out, mom_out, fuel_out, force_ref,
):
    size_x, size_y, size_z = mom_ref.shape
    rows = size_x * size_y
    total = jnp.sum(summed_ref[...], axis=0) * (1.0 / ncell)
    energy = jnp.sum(total * total)
    scaled = total * (2.0 * FORCE_POWER / (energy + ENERGY_EPS))
    coef_cos, coef_sin = scaled[0:1], scaled[1:2]
    cos_xy = cos_ref[...].reshape(rows, LANES)
    sin_xy = sin_ref[...].reshape(rows, LANES)
    side = jnp.concatenate(
        [coef_cos * cos_xy + coef_sin * sin_xy, coef_sin * cos_xy - coef_cos * sin_xy], axis=1
    )
    force_ref[...] = lax.dot_general(
        side, depth_ref[...], (((1,), (1,)), ((), ())), precision=HIGHEST,
        preferred_element_type=jnp.float32,
    ).reshape(size_x, size_y, size_z)
    gap = jnp.zeros((56, rows), jnp.float32)
    before, after = zbefore_ref[...], zafter_ref[...]
    turned = jnp.concatenate(
        [after[0:4], gap, before[4:8], after[4:8], gap, before[0:4]], axis=0
    ).T
    halo = [turned, pltpu.roll(turned, 64, 1)]
    lane = lax.broadcasted_iota(jnp.int32, (1, size_z), 1)
    dens, mom, fuel = (
        [xbefore_ref[n, i] for i in range(4)] + [ref[i] for i in range(size_x)] + [xafter_ref[n, i] for i in range(4)]
        for n, ref in enumerate((dens_ref, mom_ref, fuel_ref))
    )
    vel = [m / d for m, d in zip(mom, dens)]
    mom_flux = [m * v + d for m, v, d in zip(mom, vel, dens)]
    fuel_flux = [f * v for f, v in zip(fuel, vel)]
    for i in range(size_x):
        at = i + 4
        dens_out[i] = -first_diff(mom, at)
        spread = []
        for n, planes in enumerate((mom, fuel)):
            here = planes[at]
            tall = jnp.concatenate([ybefore_ref[n, i], here, yafter_ref[n, i]], axis=0)
            edge = halo[n][i * size_y : (i + 1) * size_y]

            def along_z(offset):
                if offset == 0:
                    return here
                if offset > 0:
                    return pltpu.roll(jnp.where(lane < offset, edge, here), size_z - offset, 1)
                return pltpu.roll(jnp.where(lane >= size_z + offset, edge, here), -offset, 1)

            spread.append(
                second_diff(lambda o: planes[at + o])
                + second_diff(lambda o: tall[4 + o : 4 + o + size_y])
                + second_diff(along_z)
            )
        mom_out[i] = -first_diff(mom_flux, at) + VISCOSITY * spread[0] + dens[at] * force_ref[i]
        fuel_out[i] = (
            -first_diff(fuel_flux, at) + DIFFUSIVITY * spread[1]
            - fuel[at] * jnp.exp(-ACTIVATION * fuel[at] / dens[at])
        )


def final_rates(density, momentum, hydrogen, summed, cos, sin, depth, halos, ncell):
    shape = density.shape
    return pl.pallas_call(
        functools.partial(final_kernel, ncell),
        out_shape=[jax.ShapeDtypeStruct(shape, jnp.float32)] * 3,
        in_specs=[VMEM] * 13,
        out_specs=[VMEM] * 3,
        scratch_shapes=[pltpu.VMEM(shape, jnp.float32)],
        compiler_params=pltpu.CompilerParams(vmem_limit_bytes=16 << 20),
        name="final_rates",
    )(density, momentum, hydrogen, summed, cos, sin, depth, *halos)


def shift_up(x, axes):
    size = lax.axis_size(axes)
    return lax.ppermute(x, axes, [(i, (i + 1) % size) for i in range(size)])


def shift_down(x, axes):
    size = lax.axis_size(axes)
    return lax.ppermute(x, axes, [((i + 1) % size, i) for i in range(size)])


def exchange(x, axes):
    return lax.all_to_all(x, axes, 0, 0, tiled=True)


def per_device(density, momentum, hydrogen, forced_modes):
    size_x, size_y, size_z = density.shape
    full = (
        size_x * lax.axis_size(GX),
        size_y * lax.axis_size(GY),
        size_z * lax.axis_size(GZ),
    )
    first, second = lax.axis_size(FIRST_GROUP), lax.axis_size(SECOND_GROUP)
    part, cos, sin, depth, xlo, xhi, ylo, yhi, zlo, zhi = partial_sums(
        density, momentum, hydrogen, forced_modes, full, first
    )
    halos = (
        shift_up(xhi, GX), shift_down(xlo, GX),
        shift_up(yhi, GY), shift_down(ylo, GY),
        shift_up(zhi, GZ), shift_down(zlo, GZ),
    )
    plane = jnp.sum(exchange(part, FIRST_GROUP), axis=0)
    summed = exchange(jnp.broadcast_to(plane[None], (second,) + plane.shape), SECOND_GROUP)
    return tuple(
        final_rates(
            density, momentum, hydrogen, summed, cos, sin, depth, halos,
            float(full[0] * full[1] * full[2]),
        )
    )


def solution(mesh):
    split = Mesh(
        mesh.devices.reshape(8, 2, 4, 2, mesh.shape["gz"]), ("gx_0", "gx_1", "gy_0", "gy_1", "gz")
    )
    field = P(GX, GY, "gz")
    return jax.shard_map(
        per_device, mesh=split, in_specs=(field, field, field, P()),
        out_specs=(field, field, field), check_vma=False,
    )
```

time: 133 us -> 81.4 us (0.61)
  the two profiles are of different devices: /device:TPU:8 before, /device:TPU:2 now
where the time goes in v1:
time: 81.4 us; the launch traced here: 80.9 us
  starting transfers between devices  38.7 us (48%)
  blocking collectives  24.6 us (30%)
  waiting for transfers between devices  11.1 us (14%)
  local copies, waits for them, and re-layouts  3.93 us (5%)
  Pallas kernels  1.77 us (2%)
    all_to_all x1, blocking collectives, exchange(): return lax.all_to_all(x, axes, 0, 0, tiled=True)  24.6 us
    ppermute x3, starting transfers between devices, shift_up(): return lax.ppermute(x, axes, [(i, (i + 1) % size) for i in range(size)])  16.4 us
    all_to_all x1, starting transfers between devices, exchange(): return lax.all_to_all(x, axes, 0, 0, tiled=True)  13.3 us
    ppermute x3, starting transfers between devices, shift_down(): return lax.ppermute(x, axes, [((i + 1) % size, i) for i in range(size)])  8.94 us
    ppermute x3, waiting for transfers between devices, shift_up(): return lax.ppermute(x, axes, [(i, (i + 1) % size) for i in range(size)])  8.87 us
    unnamed x13, local copies, waits for them, and re-layouts  3.31 us
    ppermute x3, waiting for transfers between devices, shift_down(): return lax.ppermute(x, axes, [((i + 1) % size, i) for i in range(size)])  2.26 us
  transfers between devices with their start and end apart: 7, of which 2 were waited for; matrix products, arithmetic and copies ran while one was open for 0% of the time, Pallas kernels for 0%

profile of v1, /device:TPU:2, one launch (start us, length us, event | category | flops | bytes accessed | tf_op | source)
XLA Modules:
  0.0 80.9 jit_solution(10735588960136925278)
XLA Ops:
  0.6 0.8 copy.7.modes_ref
  1.4 0.0 copy-start
  1.4 0.8 %copy-done = f32[8,16,128]{2,1,0:T(8,128)S(1)} copy-done((f32[8,16,128]{2,1,0:T(8,128)S(1)}, f32[8,16,128]{2,1,0:T(8,128)}, u32[]{:S(2)}) %copy-start) | copy-done | bytes 65560
  2.2 0.0 copy-start.2
  2.3 0.8 %copy-done.2 = f32[8,16,128]{2,1,0:T(8,128)S(1)} copy-done((f32[8,16,128]{2,1,0:T(8,128)S(1)}, f32[8,16,128]{2,1,0:T(8,128)}, u32[]{:S(2)}) %copy-start.2) | copy-done | bytes 65560
  3.1 0.0 copy-start.4
  3.1 0.8 %copy-done.4 = f32[8,16,128]{2,1,0:T(8,128)S(1)} copy-done((f32[8,16,128]{2,1,0:T(8,128)S(1)}, f32[8,16,128]{2,1,0:T(8,128)}, u32[]{:S(2)}) %copy-start.4) | copy-done | bytes 65560
  3.9 0.4 partial_sums.1
  4.4 0.0 copy-start.5
  4.4 24.6 %all_to_all.10 = f32[32,2,128]{2,1,0:T(2,128)S(1)} all-to-all(f32[32,2,128]{2,1,0:T(2,128)S(1)} %get-tuple-element.13), channel_id=1, replica_groups=mesh['gx_0'=8,'gx_1'=2,'gy_0'=4,'gy_1'=2,'gz'=8] {'gx_0','gy_0'}, dimensions={0} | all-to-all | bytes 65536 | tf_op jit(solution)/shard_map/all_to_all | solution.py:229
  29.0 0.0 copy-start.3
  29.1 0.0 copy-start.1
  29.1 0.6 broadcast_in_dim.2
  29.7 13.3 %all-to-all-start.1 = ((f32[32,2,128]{2,1,0:T(2,128)}), f32[32,2,128]{2,1,0:T(2,128)S(1)}, u32[]{:S(2)}, u32[]{:S(2)}) async-start(f32[32,2,128]{2,1,0:T(2,128)} %broadcast_in_dim.2), calls=%async_computation.1 | async-start | bytes 65536 | tf_op jit(solution)/shard_map/all_to_all | solution.py:229
  43.0 0.3 collective-permute-start
  43.3 2.7 %collective-permute-start.1 = (f32[3,4,16,128]{3,2,1,0:T(8,128)S(1)}, f32[3,4,16,128]{3,2,1,0:T(8,128)S(1)}, u32[]{:S(2)}, u32[]{:S(2)}) collective-permute-start(f32[3,4,16,128]{3,2,1,0:T(8,128)S(1)} %get-tuple-element.18), channel_id=1, source_target_pairs={{64,0},{128,64},{192,128},{256,192},{320,256},{384,320},{448,384},... | collective-permute-start | bytes 294920 | tf_op jit(solution)/shard_map/ppermute | solution.py:225
  46.0 12.4 %collective-permute-start.2 = (f32[2,8,4,128]{3,2,1,0:T(4,128)S(1)}, f32[2,8,4,128]{3,2,1,0:T(4,128)S(1)}, u32[]{:S(2)}, u32[]{:S(2)}) collective-permute-start(f32[2,8,4,128]{3,2,1,0:T(4,128)S(1)} %get-tuple-element.19), channel_id=1, source_target_pairs={{0,8},{8,16},{16,24},{24,32},{32,40},{40,48},{48,56},{56,0},{1,9},... | collective-permute-start | bytes 98312 | tf_op jit(solution)/shard_map/ppermute | solution.py:220
  58.4 3.0 %collective-permute-start.3 = (f32[2,8,4,128]{3,2,1,0:T(4,128)S(1)}, f32[2,8,4,128]{3,2,1,0:T(4,128)S(1)}, u32[]{:S(2)}, u32[]{:S(2)}) collective-permute-start(f32[2,8,4,128]{3,2,1,0:T(4,128)S(1)} %get-tuple-element.20), channel_id=1, source_target_pairs={{8,0},{16,8},{24,16},{32,24},{40,32},{48,40},{56,48},{0,56},{9,1},... | collective-permute-start | bytes 98312 | tf_op jit(solution)/shard_map/ppermute | solution.py:225
  61.5 3.7 %collective-permute-start.4 = (f32[8,128]{1,0:T(8,128)S(1)}, f32[8,128]{1,0:T(8,128)S(1)}, u32[]{:S(2)}, u32[]{:S(2)}) collective-permute-start(f32[8,128]{1,0:T(8,128)S(1)} %get-tuple-element.21), channel_id=1, source_target_pairs={{0,1},{1,2},{2,3},{3,4},{4,5},{5,6},{6,7},{7,0},{8,9},{9,10},{10,1... | collective-permute-start | bytes 12296 | tf_op jit(solution)/shard_map/ppermute | solution.py:220
  65.2 8.9 %collective-permute-done.4.zbefore_ref = f32[8,128]{1,0:T(8,128)S(1)} collective-permute-done((f32[8,128]{1,0:T(8,128)S(1)}, f32[8,128]{1,0:T(8,128)S(1)}, u32[]{:S(2)}, u32[]{:S(2)}) %collective-permute-start.4) | collective-permute-done | bytes 4128 | tf_op jit(solution)/shard_map/ppermute | solution.py:220
  74.0 3.2 %collective-permute-start.5 = (f32[8,128]{1,0:T(8,128)S(1)}, f32[8,128]{1,0:T(8,128)S(1)}, u32[]{:S(2)}, u32[]{:S(2)}) collective-permute-start(f32[8,128]{1,0:T(8,128)S(1)} %get-tuple-element.22), channel_id=1, source_target_pairs={{1,0},{2,1},{3,2},{4,3},{5,4},{6,5},{7,6},{0,7},{9,8},{10,9},{11,1... | collective-permute-start | bytes 12296 | tf_op jit(solution)/shard_map/ppermute | solution.py:225
  77.3 2.3 %collective-permute-done.5.zafter_ref = f32[8,128]{1,0:T(8,128)S(1)} collective-permute-done((f32[8,128]{1,0:T(8,128)S(1)}, f32[8,128]{1,0:T(8,128)S(1)}, u32[]{:S(2)}, u32[]{:S(2)}) %collective-permute-start.5) | collective-permute-done | bytes 4128 | tf_op jit(solution)/shard_map/ppermute | solution.py:225
  79.5 0.0 collective-permute-done.2.ybefore_ref
  79.5 0.0 collective-permute-done.3.yafter_ref
  79.5 0.0 collective-permute-done.xbefore_ref
  79.5 0.0 collective-permute-done.1.xafter_ref
  79.6 0.0 all-to-all-done.1.summed_ref
  79.6 0.0 copy-done.5
  79.6 0.0 copy-done.3
  79.6 0.0 copy-done.1
  79.6 1.3 %final_rates.1 = (f32[8,16,128]{2,1,0:T(8,128)}, f32[8,16,128]{2,1,0:T(8,128)}, f32[8,16,128]{2,1,0:T(8,128)}) custom-call(f32[8,16,128]{2,1,0:T(8,128)S(1)} %copy-done.1, f32[8,16,128]{2,1,0:T(8,128)S(1)} %copy-done.3, f32[8,16,128]{2,1,0:T(8,128)S(1)} %copy-done.5, f32[32,2,128]{2,1,0:T(2,128)S(1)} %all-to-all-done.1.summed_ref, ...), custom_call_target="tpu_custom_call" | custom-call | tf_op jit(solution)/shard_map/final_rates/pallas_call | solution.py:207
  (1 shorter events, 0.0 us)
Async XLA Ops:
  1.4 0.8 %copy-start = (f32[8,16,128]{2,1,0:T(8,128)S(1)}, f32[8,16,128]{2,1,0:T(8,128)}, u32[]{:S(2)}) copy-start(f32[8,16,128]{2,1,0:T(8,128)} %dens_ref.3) | copy-start | bytes 196612
  2.2 0.8 %copy-start.2 = (f32[8,16,128]{2,1,0:T(8,128)S(1)}, f32[8,16,128]{2,1,0:T(8,128)}, u32[]{:S(2)}) copy-start(f32[8,16,128]{2,1,0:T(8,128)} %mom_ref.3) | copy-start | bytes 196612
  3.1 0.8 %copy-start.4 = (f32[8,16,128]{2,1,0:T(8,128)S(1)}, f32[8,16,128]{2,1,0:T(8,128)}, u32[]{:S(2)}) copy-start(f32[8,16,128]{2,1,0:T(8,128)} %fuel_ref.3) | copy-start | bytes 196612
  4.4 75.2 %copy-start.5 = (f32[8,16,128]{2,1,0:T(8,128)S(1)}, f32[8,16,128]{2,1,0:T(8,128)}, u32[]{:S(2)}) copy-start(f32[8,16,128]{2,1,0:T(8,128)} %fuel_ref.3) | copy-start | bytes 196612
  29.0 50.5 %copy-start.3 = (f32[8,16,128]{2,1,0:T(8,128)S(1)}, f32[8,16,128]{2,1,0:T(8,128)}, u32[]{:S(2)}) copy-start(f32[8,16,128]{2,1,0:T(8,128)} %mom_ref.3) | copy-start | bytes 196612
  29.1 50.5 %copy-start.1 = (f32[8,16,128]{2,1,0:T(8,128)S(1)}, f32[8,16,128]{2,1,0:T(8,128)}, u32[]{:S(2)}) copy-start(f32[8,16,128]{2,1,0:T(8,128)} %dens_ref.3) | copy-start | bytes 196612
  29.7 49.9 %all-to-all-start.1 = ((f32[32,2,128]{2,1,0:T(2,128)}), f32[32,2,128]{2,1,0:T(2,128)S(1)}, u32[]{:S(2)}, u32[]{:S(2)}) async-start(f32[32,2,128]{2,1,0:T(2,128)} %broadcast_in_dim.2), calls=%async_computation.1 | async-start | bytes 65536 | tf_op jit(solution)/shard_map/all_to_all | solution.py:229
  43.0 36.5 %collective-permute-start = (f32[3,4,16,128]{3,2,1,0:T(8,128)S(1)}, f32[3,4,16,128]{3,2,1,0:T(8,128)S(1)}, u32[]{:S(2)}, u32[]{:S(2)}) collective-permute-start(f32[3,4,16,128]{3,2,1,0:T(8,128)S(1)} %get-tuple-element.17), channel_id=1, source_target_pairs={{0,64},{64,128},{128,192},{192,256},{256,320},{320,384},{384,448},... | collective-permute-start | bytes 294920 | tf_op jit(solution)/shard_map/ppermute | solution.py:220
  43.3 36.2 %collective-permute-start.1 = (f32[3,4,16,128]{3,2,1,0:T(8,128)S(1)}, f32[3,4,16,128]{3,2,1,0:T(8,128)S(1)}, u32[]{:S(2)}, u32[]{:S(2)}) collective-permute-start(f32[3,4,16,128]{3,2,1,0:T(8,128)S(1)} %get-tuple-element.18), channel_id=1, source_target_pairs={{64,0},{128,64},{192,128},{256,192},{320,256},{384,320},{448,384},... | collective-permute-start | bytes 294920 | tf_op jit(solution)/shard_map/ppermute | solution.py:225
  46.0 33.5 %collective-permute-start.2 = (f32[2,8,4,128]{3,2,1,0:T(4,128)S(1)}, f32[2,8,4,128]{3,2,1,0:T(4,128)S(1)}, u32[]{:S(2)}, u32[]{:S(2)}) collective-permute-start(f32[2,8,4,128]{3,2,1,0:T(4,128)S(1)} %get-tuple-element.19), channel_id=1, source_target_pairs={{0,8},{8,16},{16,24},{24,32},{32,40},{40,48},{48,56},{56,0},{1,9},... | collective-permute-start | bytes 98312 | tf_op jit(solution)/shard_map/ppermute | solution.py:220
  58.4 21.1 %collective-permute-start.3 = (f32[2,8,4,128]{3,2,1,0:T(4,128)S(1)}, f32[2,8,4,128]{3,2,1,0:T(4,128)S(1)}, u32[]{:S(2)}, u32[]{:S(2)}) collective-permute-start(f32[2,8,4,128]{3,2,1,0:T(4,128)S(1)} %get-tuple-element.20), channel_id=1, source_target_pairs={{8,0},{16,8},{24,16},{32,24},{40,32},{48,40},{56,48},{0,56},{9,1},... | collective-permute-start | bytes 98312 | tf_op jit(solution)/shard_map/ppermute | solution.py:225
  61.5 12.6 %collective-permute-start.4 = (f32[8,128]{1,0:T(8,128)S(1)}, f32[8,128]{1,0:T(8,128)S(1)}, u32[]{:S(2)}, u32[]{:S(2)}) collective-permute-start(f32[8,128]{1,0:T(8,128)S(1)} %get-tuple-element.21), channel_id=1, source_target_pairs={{0,1},{1,2},{2,3},{3,4},{4,5},{5,6},{6,7},{7,0},{8,9},{9,10},{10,1... | collective-permute-start | bytes 12296 | tf_op jit(solution)/shard_map/ppermute | solution.py:220
  74.0 5.5 %collective-permute-start.5 = (f32[8,128]{1,0:T(8,128)S(1)}, f32[8,128]{1,0:T(8,128)S(1)}, u32[]{:S(2)}, u32[]{:S(2)}) collective-permute-start(f32[8,128]{1,0:T(8,128)S(1)} %get-tuple-element.22), channel_id=1, source_target_pairs={{1,0},{2,1},{3,2},{4,3},{5,4},{6,5},{7,6},{0,7},{9,8},{10,9},{11,1... | collective-permute-start | bytes 12296 | tf_op jit(solution)/shard_map/ppermute | solution.py:225

commit v2 on v1

--- a/solution.py
+++ b/solution.py
@@ -7,6 +7,7 @@
 from jax.experimental.pallas import tpu as pltpu
 from jax.sharding import Mesh
 from jax.sharding import PartitionSpec as P
+
 
 GX = ("gx_0", "gx_1")
 GY = ("gy_0", "gy_1")
@@ -27,12 +28,8 @@
 VMEM = pl.BlockSpec(memory_space=pltpu.VMEM)
 
 
-def row_of(column):
-    count = column.shape[0]
-    row = lax.broadcasted_iota(jnp.int32, (count, LANES), 0)
-    lane = lax.broadcasted_iota(jnp.int32, (count, LANES), 1)
-    spread = jnp.broadcast_to(column, (count, LANES))
-    return jnp.sum(jnp.where(row == lane, spread, 0.0), axis=0, keepdims=True)
+def odd(axis):
+    return lax.rem(lax.axis_index(axis), 2) == 1
 
 
 def angles(wave, start, step, count, total):
@@ -44,24 +41,23 @@
 
 
 def partial_kernel(
-    full, copies, dens_ref, mom_ref, fuel_ref, modes_ref,
+    full, copies, dens_hbm, mom_hbm, fuel_hbm, modes_ref,
     part_ref, cos_ref, sin_ref, depth_ref,
-    xlo_ref, xhi_ref, ylo_ref, yhi_ref, zlo_ref, zhi_ref,
+    xa_ref, xb_ref, ya_ref, yb_ref, za_ref, zb_ref,
+    dens_ref, mom_ref, fuel_ref, sems,
 ):
     size_x, size_y, size_z = mom_ref.shape
     rows = size_x * size_y
     half = 4
-    for n, ref in enumerate((dens_ref, mom_ref, fuel_ref)):
-        xlo_ref[n] = ref[0:half]
-        xhi_ref[n] = ref[size_x - half : size_x]
-    for n, ref in enumerate((mom_ref, fuel_ref)):
-        ylo_ref[n] = ref[:, 0:half, :]
-        yhi_ref[n] = ref[:, size_y - half : size_y, :]
-    turned = [ref[...].reshape(rows, size_z).T for ref in (mom_ref, fuel_ref)]
-    zlo_ref[...] = jnp.concatenate([t[0:half] for t in turned], axis=0)
-    zhi_ref[...] = jnp.concatenate([t[size_z - half : size_z] for t in turned], axis=0)
+    loads = [
+        pltpu.make_async_copy(src, dst, sems.at[n])
+        for n, (src, dst) in enumerate(((mom_hbm, mom_ref), (dens_hbm, dens_ref), (fuel_hbm, fuel_ref)))
+    ]
+    for load in loads:
+        load.start()
     modes = modes_ref[...].astype(jnp.float32)
-    wave_x, wave_y, wave_z = (row_of(modes[:, n : n + 1]) for n in range(3))
+    spare = jnp.zeros((1, LANES - modes.shape[1]), jnp.float32)
+    wave_x, wave_y, wave_z = (jnp.concatenate([modes[n : n + 1], spare], axis=1) for n in range(3))
     base_x = (lax.axis_index("gx_0") * 2 + lax.axis_index("gx_1")) * size_x
     base_y = (lax.axis_index("gy_0") * 2 + lax.axis_index("gy_1")) * size_y
     base_z = lax.axis_index("gz") * size_z
@@ -78,7 +74,7 @@
     cos, sin = jnp.cos(angle), jnp.sin(angle)
     at_y, at_z, at_f = size_x, size_x + size_y, size_x + size_y + 8
     cy, sy = cos[at_y:at_z], sin[at_y:at_z]
-    live = lax.broadcasted_iota(jnp.int32, (1, LANES), 1) < modes_ref.shape[0]
+    live = lax.broadcasted_iota(jnp.int32, (1, LANES), 1) < modes.shape[1]
     cf = jnp.where(live, cos[at_f:], 0.0)
     sf = jnp.where(live, sin[at_f:], 0.0)
     for n in range(size_x):
@@ -89,6 +85,8 @@
         cz, sz = cos[at_z + n : at_z + n + 1], sin[at_z + n : at_z + n + 1]
         depth_ref[n * fine : (n + 1) * fine, 0:LANES] = cz * cf - sz * sf
         depth_ref[n * fine : (n + 1) * fine, LANES:] = sz * cf + cz * sf
+    loads[0].wait()
+    loads[1].wait()
     velocity = (mom_ref[...] / dens_ref[...]).reshape(rows, size_z)
     along = jnp.dot(velocity, depth_ref[...], precision=HIGHEST, preferred_element_type=jnp.float32)
     real, imag = along[:, 0:LANES], along[:, LANES:]
@@ -98,6 +96,21 @@
     part_sin = jnp.sum(sin_xy * real + cos_xy * imag, axis=0, keepdims=True)
     both = jnp.concatenate([part_cos, part_sin], axis=0)
     part_ref[...] = jnp.broadcast_to(both[None], (copies, 2, LANES))
+    loads[2].wait()
+    odd_x, odd_y, odd_z = odd("gx_1"), odd("gy_1"), odd("gz")
+    for n, ref in enumerate((dens_ref, mom_ref, fuel_ref)):
+        low, high = ref[0:half], ref[size_x - half : size_x]
+        xa_ref[n] = jnp.where(odd_x, low, high)
+        xb_ref[n] = jnp.where(odd_x, high, low)
+    for n, ref in enumerate((mom_ref, fuel_ref)):
+        low, high = ref[:, 0:half, :], ref[:, size_y - half : size_y, :]
+        ya_ref[n] = jnp.where(odd_y, low, high)
+        yb_ref[n] = jnp.where(odd_y, high, low)
+    turned = [ref[...].reshape(rows, size_z).T for ref in (mom_ref, fuel_ref)]
+    low = jnp.concatenate([t[0:half] for t in turned], axis=0)
+    high = jnp.concatenate([t[size_z - half : size_z] for t in turned], axis=0)
+    za_ref[...] = jnp.where(odd_z, low, high)
+    zb_ref[...] = jnp.where(odd_z, high, low)
 
 
 def partial_sums(density, momentum, hydrogen, modes, full, copies):
@@ -118,11 +131,27 @@
     return pl.pallas_call(
         functools.partial(partial_kernel, full, copies),
         out_shape=[jax.ShapeDtypeStruct(s, f32) for s in shapes],
-        in_specs=[VMEM] * 4,
+        in_specs=[pl.BlockSpec(memory_space=pltpu.HBM)] * 3 + [VMEM],
         out_specs=[VMEM] * len(shapes),
+        scratch_shapes=[pltpu.VMEM(density.shape, f32)] * 3 + [pltpu.SemaphoreType.DMA((3,))],
         compiler_params=pltpu.CompilerParams(vmem_limit_bytes=16 << 20),
         name="partial_sums",
     )(density, momentum, hydrogen, modes)
+
+
+def spread_kernel(parts_ref, out_ref):
+    out_ref[...] = jnp.broadcast_to(jnp.sum(parts_ref[...], axis=0, keepdims=True), out_ref.shape)
+
+
+def summed_copies(parts, copies):
+    return pl.pallas_call(
+        spread_kernel,
+        out_shape=jax.ShapeDtypeStruct((copies,) + parts.shape[1:], jnp.float32),
+        in_specs=[VMEM],
+        out_specs=VMEM,
+        compiler_params=pltpu.CompilerParams(vmem_limit_bytes=4 << 20),
+        name="summed_copies",
+    )(parts)
 
 
 def first_diff(planes, at):
@@ -142,7 +171,7 @@
 
 def final_kernel(
     ncell, dens_ref, mom_ref, fuel_ref, summed_ref, cos_ref, sin_ref, depth_ref,
-    xbefore_ref, xafter_ref, ybefore_ref, yafter_ref, zbefore_ref, zafter_ref,
+    xa_ref, xb_ref, ya_ref, yb_ref, za_ref, zb_ref,
     dens_out, mom_out, fuel_out, force_ref,
 ):
     size_x, size_y, size_z = mom_ref.shape
@@ -161,14 +190,18 @@
         preferred_element_type=jnp.float32,
     ).reshape(size_x, size_y, size_z)
     gap = jnp.zeros((56, rows), jnp.float32)
-    before, after = zbefore_ref[...], zafter_ref[...]
+    odd_x, odd_y, odd_z = odd("gx_1"), odd("gy_1"), odd("gz")
+    before = jnp.where(odd_z, za_ref[...], zb_ref[...])
+    after = jnp.where(odd_z, zb_ref[...], za_ref[...])
     turned = jnp.concatenate(
         [after[0:4], gap, before[4:8], after[4:8], gap, before[0:4]], axis=0
     ).T
     halo = [turned, pltpu.roll(turned, 64, 1)]
     lane = lax.broadcasted_iota(jnp.int32, (1, size_z), 1)
     dens, mom, fuel = (
-        [xbefore_ref[n, i] for i in range(4)] + [ref[i] for i in range(size_x)] + [xafter_ref[n, i] for i in range(4)]
+        [jnp.where(odd_x, xa_ref[n, i], xb_ref[n, i]) for i in range(4)]
+        + [ref[i] for i in range(size_x)]
+        + [jnp.where(odd_x, xb_ref[n, i], xa_ref[n, i]) for i in range(4)]
         for n, ref in enumerate((dens_ref, mom_ref, fuel_ref))
     )
     vel = [m / d for m, d in zip(mom, dens)]
@@ -180,7 +213,8 @@
         spread = []
         for n, planes in enumerate((mom, fuel)):
             here = planes[at]
-            tall = jnp.concatenate([ybefore_ref[n, i], here, yafter_ref[n, i]], axis=0)
+            ya, yb = ya_ref[n, i], yb_ref[n, i]
+            tall = jnp.concatenate([jnp.where(odd_y, ya, yb), here, jnp.where(odd_y, yb, ya)], axis=0)
             edge = halo[n][i * size_y : (i + 1) * size_y]
 
             def along_z(offset):
@@ -215,14 +249,10 @@
     )(density, momentum, hydrogen, summed, cos, sin, depth, *halos)
 
 
-def shift_up(x, axes):
+def swap(x, axes, shift):
     size = lax.axis_size(axes)
-    return lax.ppermute(x, axes, [(i, (i + 1) % size) for i in range(size)])
-
-
-def shift_down(x, axes):
-    size = lax.axis_size(axes)
-    return lax.ppermute(x, axes, [((i + 1) % size, i) for i in range(size)])
+    pairs = [((i + shift) % size, (i + 1 + shift) % size) for i in range(0, size, 2)]
+    return lax.ppermute(x, axes, pairs + [(j, i) for i, j in pairs])
 
 
 def exchange(x, axes):
@@ -237,22 +267,20 @@
         size_z * lax.axis_size(GZ),
     )
     first, second = lax.axis_size(FIRST_GROUP), lax.axis_size(SECOND_GROUP)
-    part, cos, sin, depth, xlo, xhi, ylo, yhi, zlo, zhi = partial_sums(
-        density, momentum, hydrogen, forced_modes, full, first
-    )
-    halos = (
-        shift_up(xhi, GX), shift_down(xlo, GX),
-        shift_up(yhi, GY), shift_down(ylo, GY),
-        shift_up(zhi, GZ), shift_down(zlo, GZ),
-    )
-    plane = jnp.sum(exchange(part, FIRST_GROUP), axis=0)
-    summed = exchange(jnp.broadcast_to(plane[None], (second,) + plane.shape), SECOND_GROUP)
-    return tuple(
-        final_rates(
-            density, momentum, hydrogen, summed, cos, sin, depth, halos,
-            float(full[0] * full[1] * full[2]),
-        )
-    )
+    part, cos, sin, depth, xa, xb, ya, yb, za, zb = partial_sums(
+        density, momentum, hydrogen, forced_modes.T, full, first
+    )
+    part = exchange(part, FIRST_GROUP)
+    ya, yb = swap(ya, GY, 0), swap(yb, GY, 1)
+    part = summed_copies(part, second)
+    part = exchange(part, SECOND_GROUP)
+    xa, xb = swap(xa, GX, 0), swap(xb, GX, 1)
+    za, zb = swap(za, GZ, 0), swap(zb, GZ, 1)
+    rates = final_rates(
+        density, momentum, hydrogen, part, cos, sin, depth, (xa, xb, ya, yb, za, zb),
+        float(full[0] * full[1] * full[2]),
+    )
+    return tuple(rates)
 
 
 def solution(mesh):

time: 81.4 us -> 83.5 us (1.026)
  the two profiles are of different devices: /device:TPU:2 before, /device:TPU:8 now
where the time goes in v2:
time: 83.5 us; the launch traced here: 82.9 us
  starting transfers between devices  47.9 us (57%)
  blocking collectives  24.6 us (29%)
  waiting for transfers between devices  3.68 us (4%)
  local copies, waits for them, and re-layouts  3.21 us (4%)
  Pallas kernels  2.76 us (3%)
    ppermute x6, starting transfers between devices, swap(): return lax.ppermute(x, axes, pairs + [(j, i) for i, j in pairs])  34.6 us
    all_to_all x1, blocking collectives, exchange(): return lax.all_to_all(x, axes, 0, 0, tiled=True)  24.6 us
    all_to_all x1, starting transfers between devices, exchange(): return lax.all_to_all(x, axes, 0, 0, tiled=True)  13.3 us
    ppermute x6, waiting for transfers between devices, swap(): return lax.ppermute(x, axes, pairs + [(j, i) for i, j in pairs])  3.68 us
    unnamed x14, local copies, waits for them, and re-layouts  3.21 us
  transfers between devices with their start and end apart: 7, of which 2 were waited for; matrix products, arithmetic and copies ran while one was open for 0% of the time, Pallas kernels for 0%

profile of v2, /device:TPU:8, one launch (start us, length us, event | category | flops | bytes accessed | tf_op | source)
XLA Modules:
  0.0 82.9 jit_solution(4610447498618421104)
XLA Ops:
  0.6 0.0 copy-start
  0.6 0.8 %copy-done = f32[8,16,128]{2,1,0:T(8,128)S(1)} copy-done((f32[8,16,128]{2,1,0:T(8,128)S(1)}, f32[8,16,128]{2,1,0:T(8,128)}, u32[]{:S(2)}) %copy-start) | copy-done | bytes 65560
  1.5 0.0 copy-start.2
  1.5 0.8 %copy-done.2 = f32[8,16,128]{2,1,0:T(8,128)S(1)} copy-done((f32[8,16,128]{2,1,0:T(8,128)S(1)}, f32[8,16,128]{2,1,0:T(8,128)}, u32[]{:S(2)}) %copy-start.2) | copy-done | bytes 65560
  2.3 0.0 copy-start.4
  2.3 0.8 %copy-done.4 = f32[8,16,128]{2,1,0:T(8,128)S(1)} copy-done((f32[8,16,128]{2,1,0:T(8,128)S(1)}, f32[8,16,128]{2,1,0:T(8,128)}, u32[]{:S(2)}) %copy-start.4) | copy-done | bytes 65560
  3.2 0.0 copy-start.6
  3.2 0.7 copy-done.6
  3.8 0.8 partial_sums.1
  4.6 0.0 copy-start.5
  4.6 24.6 %all_to_all.10.parts_ref = f32[32,2,128]{2,1,0:T(2,128)S(1)} all-to-all(f32[32,2,128]{2,1,0:T(2,128)S(1)} %get-tuple-element.13), channel_id=1, replica_groups=mesh['gx_0'=8,'gx_1'=2,'gy_0'=4,'gy_1'=2,'gz'=8] {'gx_0','gy_0'}, dimensions={0} | all-to-all | bytes 65536 | tf_op jit(solution)/shard_map/all_to_all | solution.py:259
  29.2 0.0 copy-start.1
  29.2 0.0 copy-start.3
  29.2 0.7 summed_copies.1
  29.9 13.3 %all-to-all-start.1 = ((f32[32,2,128]{2,1,0:T(2,128)}), f32[32,2,128]{2,1,0:T(2,128)S(1)}, u32[]{:S(2)}, u32[]{:S(2)}) async-start(f32[32,2,128]{2,1,0:T(2,128)} %summed_copies.1), calls=%async_computation.1 | async-start | bytes 65536 | tf_op jit(solution)/shard_map/all_to_all | solution.py:259
  43.2 2.2 %collective-permute-start = (f32[3,4,16,128]{3,2,1,0:T(8,128)S(1)}, f32[3,4,16,128]{3,2,1,0:T(8,128)S(1)}, u32[]{:S(2)}, u32[]{:S(2)}) collective-permute-start(f32[3,4,16,128]{3,2,1,0:T(8,128)S(1)} %get-tuple-element.17), channel_id=1, source_target_pairs={{0,64},{128,192},{256,320},{384,448},{512,576},{640,704},{768,832}... | collective-permute-start | bytes 294920 | tf_op jit(solution)/shard_map/ppermute | solution.py:255
  45.4 3.1 %collective-permute-start.1 = (f32[3,4,16,128]{3,2,1,0:T(8,128)S(1)}, f32[3,4,16,128]{3,2,1,0:T(8,128)S(1)}, u32[]{:S(2)}, u32[]{:S(2)}) collective-permute-start(f32[3,4,16,128]{3,2,1,0:T(8,128)S(1)} %get-tuple-element.18), channel_id=1, source_target_pairs={{64,128},{192,256},{320,384},{448,512},{576,640},{704,768},{832,89... | collective-permute-start | bytes 294920 | tf_op jit(solution)/shard_map/ppermute | solution.py:255
  48.6 12.4 %collective-permute-start.2 = (f32[2,8,4,128]{3,2,1,0:T(4,128)S(1)}, f32[2,8,4,128]{3,2,1,0:T(4,128)S(1)}, u32[]{:S(2)}, u32[]{:S(2)}) collective-permute-start(f32[2,8,4,128]{3,2,1,0:T(4,128)S(1)} %get-tuple-element.19), channel_id=1, source_target_pairs={{0,8},{16,24},{32,40},{48,56},{8,0},{24,16},{40,32},{56,48},{1,9},... | collective-permute-start | bytes 98312 | tf_op jit(solution)/shard_map/ppermute | solution.py:255
  61.0 2.9 %collective-permute-start.3 = (f32[2,8,4,128]{3,2,1,0:T(4,128)S(1)}, f32[2,8,4,128]{3,2,1,0:T(4,128)S(1)}, u32[]{:S(2)}, u32[]{:S(2)}) collective-permute-start(f32[2,8,4,128]{3,2,1,0:T(4,128)S(1)} %get-tuple-element.20), channel_id=1, source_target_pairs={{8,16},{24,32},{40,48},{56,0},{16,8},{32,24},{48,40},{0,56},{9,17}... | collective-permute-start | bytes 98312 | tf_op jit(solution)/shard_map/ppermute | solution.py:255
  63.9 3.7 %collective-permute-start.4 = (f32[8,128]{1,0:T(8,128)S(1)}, f32[8,128]{1,0:T(8,128)S(1)}, u32[]{:S(2)}, u32[]{:S(2)}) collective-permute-start(f32[8,128]{1,0:T(8,128)S(1)} %get-tuple-element.21), channel_id=1, source_target_pairs={{0,1},{2,3},{4,5},{6,7},{1,0},{3,2},{5,4},{7,6},{8,9},{10,11},{12,... | collective-permute-start | bytes 12296 | tf_op jit(solution)/shard_map/ppermute | solution.py:255
  67.6 1.8 %collective-permute-done.4.za_ref = f32[8,128]{1,0:T(8,128)S(1)} collective-permute-done((f32[8,128]{1,0:T(8,128)S(1)}, f32[8,128]{1,0:T(8,128)S(1)}, u32[]{:S(2)}, u32[]{:S(2)}) %collective-permute-start.4) | collective-permute-done | bytes 4128 | tf_op jit(solution)/shard_map/ppermute | solution.py:255
  69.4 10.3 %collective-permute-start.5 = (f32[8,128]{1,0:T(8,128)S(1)}, f32[8,128]{1,0:T(8,128)S(1)}, u32[]{:S(2)}, u32[]{:S(2)}) collective-permute-start(f32[8,128]{1,0:T(8,128)S(1)} %get-tuple-element.22), channel_id=1, source_target_pairs={{1,2},{3,4},{5,6},{7,0},{2,1},{4,3},{6,5},{0,7},{9,10},{11,12},{13... | collective-permute-start | bytes 12296 | tf_op jit(solution)/shard_map/ppermute | solution.py:255
  79.7 1.8 %collective-permute-done.5.zb_ref = f32[8,128]{1,0:T(8,128)S(1)} collective-permute-done((f32[8,128]{1,0:T(8,128)S(1)}, f32[8,128]{1,0:T(8,128)S(1)}, u32[]{:S(2)}, u32[]{:S(2)}) %collective-permute-start.5) | collective-permute-done | bytes 4128 | tf_op jit(solution)/shard_map/ppermute | solution.py:255
  81.5 0.0 collective-permute-done.2.ya_ref
  81.5 0.0 collective-permute-done.3.yb_ref
  81.5 0.0 collective-permute-done.xa_ref
  81.5 0.0 collective-permute-done.1.xb_ref
  81.6 0.0 all-to-all-done.1.summed_ref
  81.6 0.0 copy-done.5
  81.6 0.0 copy-done.1
  81.6 0.0 copy-done.3
  81.6 1.3 %final_rates.1 = (f32[8,16,128]{2,1,0:T(8,128)}, f32[8,16,128]{2,1,0:T(8,128)}, f32[8,16,128]{2,1,0:T(8,128)}) custom-call(f32[8,16,128]{2,1,0:T(8,128)S(1)} %copy-done.1, f32[8,16,128]{2,1,0:T(8,128)S(1)} %copy-done.3, f32[8,16,128]{2,1,0:T(8,128)S(1)} %copy-done.5, f32[32,2,128]{2,1,0:T(2,128)S(1)} %all-to-all-done.1.summed_ref, ...), custom_call_target="tpu_custom_call" | custom-call | tf_op jit(solution)/shard_map/final_rates/pallas_call | solution.py:241
Async XLA Ops:
  0.6 0.8 %copy-start = (f32[8,16,128]{2,1,0:T(8,128)S(1)}, f32[8,16,128]{2,1,0:T(8,128)}, u32[]{:S(2)}) copy-start(f32[8,16,128]{2,1,0:T(8,128)} %dens_ref.1) | copy-start | bytes 196612
  1.5 0.8 %copy-start.2 = (f32[8,16,128]{2,1,0:T(8,128)S(1)}, f32[8,16,128]{2,1,0:T(8,128)}, u32[]{:S(2)}) copy-start(f32[8,16,128]{2,1,0:T(8,128)} %mom_ref.1) | copy-start | bytes 196612
  2.3 0.8 %copy-start.4 = (f32[8,16,128]{2,1,0:T(8,128)S(1)}, f32[8,16,128]{2,1,0:T(8,128)}, u32[]{:S(2)}) copy-start(f32[8,16,128]{2,1,0:T(8,128)} %fuel_ref.1) | copy-start | bytes 196612
  3.2 0.7 copy-start.6
  4.6 77.0 %copy-start.5 = (f32[8,16,128]{2,1,0:T(8,128)S(1)}, f32[8,16,128]{2,1,0:T(8,128)}, u32[]{:S(2)}) copy-start(f32[8,16,128]{2,1,0:T(8,128)} %fuel_ref.1) | copy-start | bytes 196612
  29.2 52.3 %copy-start.1 = (f32[8,16,128]{2,1,0:T(8,128)S(1)}, f32[8,16,128]{2,1,0:T(8,128)}, u32[]{:S(2)}) copy-start(f32[8,16,128]{2,1,0:T(8,128)} %dens_ref.1) | copy-start | bytes 196612
  29.2 52.3 %copy-start.3 = (f32[8,16,128]{2,1,0:T(8,128)S(1)}, f32[8,16,128]{2,1,0:T(8,128)}, u32[]{:S(2)}) copy-start(f32[8,16,128]{2,1,0:T(8,128)} %mom_ref.1) | copy-start | bytes 196612
  29.9 51.7 %all-to-all-start.1 = ((f32[32,2,128]{2,1,0:T(2,128)}), f32[32,2,128]{2,1,0:T(2,128)S(1)}, u32[]{:S(2)}, u32[]{:S(2)}) async-start(f32[32,2,128]{2,1,0:T(2,128)} %summed_copies.1), calls=%async_computation.1 | async-start | bytes 65536 | tf_op jit(solution)/shard_map/all_to_all | solution.py:259
  43.2 38.3 %collective-permute-start = (f32[3,4,16,128]{3,2,1,0:T(8,128)S(1)}, f32[3,4,16,128]{3,2,1,0:T(8,128)S(1)}, u32[]{:S(2)}, u32[]{:S(2)}) collective-permute-start(f32[3,4,16,128]{3,2,1,0:T(8,128)S(1)} %get-tuple-element.17), channel_id=1, source_target_pairs={{0,64},{128,192},{256,320},{384,448},{512,576},{640,704},{768,832}... | collective-permute-start | bytes 294920 | tf_op jit(solution)/shard_map/ppermute | solution.py:255
  45.4 36.1 %collective-permute-start.1 = (f32[3,4,16,128]{3,2,1,0:T(8,128)S(1)}, f32[3,4,16,128]{3,2,1,0:T(8,128)S(1)}, u32[]{:S(2)}, u32[]{:S(2)}) collective-permute-start(f32[3,4,16,128]{3,2,1,0:T(8,128)S(1)} %get-tuple-element.18), channel_id=1, source_target_pairs={{64,128},{192,256},{320,384},{448,512},{576,640},{704,768},{832,89... | collective-permute-start | bytes 294920 | tf_op jit(solution)/shard_map/ppermute | solution.py:255
  48.6 33.0 %collective-permute-start.2 = (f32[2,8,4,128]{3,2,1,0:T(4,128)S(1)}, f32[2,8,4,128]{3,2,1,0:T(4,128)S(1)}, u32[]{:S(2)}, u32[]{:S(2)}) collective-permute-start(f32[2,8,4,128]{3,2,1,0:T(4,128)S(1)} %get-tuple-element.19), channel_id=1, source_target_pairs={{0,8},{16,24},{32,40},{48,56},{8,0},{24,16},{40,32},{56,48},{1,9},... | collective-permute-start | bytes 98312 | tf_op jit(solution)/shard_map/ppermute | solution.py:255
  61.0 20.5 %collective-permute-start.3 = (f32[2,8,4,128]{3,2,1,0:T(4,128)S(1)}, f32[2,8,4,128]{3,2,1,0:T(4,128)S(1)}, u32[]{:S(2)}, u32[]{:S(2)}) collective-permute-start(f32[2,8,4,128]{3,2,1,0:T(4,128)S(1)} %get-tuple-element.20), channel_id=1, source_target_pairs={{8,16},{24,32},{40,48},{56,0},{16,8},{32,24},{48,40},{0,56},{9,17}... | collective-permute-start | bytes 98312 | tf_op jit(solution)/shard_map/ppermute | solution.py:255
  63.9 5.5 %collective-permute-start.4 = (f32[8,128]{1,0:T(8,128)S(1)}, f32[8,128]{1,0:T(8,128)S(1)}, u32[]{:S(2)}, u32[]{:S(2)}) collective-permute-start(f32[8,128]{1,0:T(8,128)S(1)} %get-tuple-element.21), channel_id=1, source_target_pairs={{0,1},{2,3},{4,5},{6,7},{1,0},{3,2},{5,4},{7,6},{8,9},{10,11},{12,... | collective-permute-start | bytes 12296 | tf_op jit(solution)/shard_map/ppermute | solution.py:255
  69.4 12.1 %collective-permute-start.5 = (f32[8,128]{1,0:T(8,128)S(1)}, f32[8,128]{1,0:T(8,128)S(1)}, u32[]{:S(2)}, u32[]{:S(2)}) collective-permute-start(f32[8,128]{1,0:T(8,128)S(1)} %get-tuple-element.22), channel_id=1, source_target_pairs={{1,2},{3,4},{5,6},{7,0},{2,1},{4,3},{6,5},{0,7},{9,10},{11,12},{13... | collective-permute-start | bytes 12296 | tf_op jit(solution)/shard_map/ppermute | solution.py:255

commit v3 on v2

--- a/solution.py
+++ b/solution.py
@@ -13,6 +13,7 @@
 GY = ("gy_0", "gy_1")
 GZ = ("gz",)
 FIRST_GROUP = ("gx_0", "gy_0")
+RING = ("gy_1", "gz")
 SECOND_GROUP = ("gx_1", "gy_1", "gz")
 
 FIRST_COEFFS = (0.8, -0.2, 4.0 / 105.0, -1.0 / 280.0)
@@ -41,20 +42,23 @@
 
 
 def partial_kernel(
-    full, copies, dens_hbm, mom_hbm, fuel_hbm, modes_ref,
+    full, copies, dens_hbm, mom_hbm, fuel_hbm, modes_hbm,
     part_ref, cos_ref, sin_ref, depth_ref,
-    xa_ref, xb_ref, ya_ref, yb_ref, za_ref, zb_ref,
-    dens_ref, mom_ref, fuel_ref, sems,
+    xa_ref, xb_ref, sides_ref, za_ref, zb_ref,
+    dens_ref, mom_ref, fuel_ref, modes_ref, sems,
 ):
     size_x, size_y, size_z = mom_ref.shape
     rows = size_x * size_y
     half = 4
     loads = [
         pltpu.make_async_copy(src, dst, sems.at[n])
-        for n, (src, dst) in enumerate(((mom_hbm, mom_ref), (dens_hbm, dens_ref), (fuel_hbm, fuel_ref)))
+        for n, (src, dst) in enumerate(
+            ((modes_hbm, modes_ref), (mom_hbm, mom_ref), (dens_hbm, dens_ref), (fuel_hbm, fuel_ref))
+        )
     ]
     for load in loads:
         load.start()
+    loads[0].wait()
     modes = modes_ref[...].astype(jnp.float32)
     spare = jnp.zeros((1, LANES - modes.shape[1]), jnp.float32)
     wave_x, wave_y, wave_z = (jnp.concatenate([modes[n : n + 1], spare], axis=1) for n in range(3))
@@ -85,8 +89,8 @@
         cz, sz = cos[at_z + n : at_z + n + 1], sin[at_z + n : at_z + n + 1]
         depth_ref[n * fine : (n + 1) * fine, 0:LANES] = cz * cf - sz * sf
         depth_ref[n * fine : (n + 1) * fine, LANES:] = sz * cf + cz * sf
-    loads[0].wait()
     loads[1].wait()
+    loads[2].wait()
     velocity = (mom_ref[...] / dens_ref[...]).reshape(rows, size_z)
     along = jnp.dot(velocity, depth_ref[...], precision=HIGHEST, preferred_element_type=jnp.float32)
     real, imag = along[:, 0:LANES], along[:, LANES:]
@@ -96,7 +100,7 @@
     part_sin = jnp.sum(sin_xy * real + cos_xy * imag, axis=0, keepdims=True)
     both = jnp.concatenate([part_cos, part_sin], axis=0)
     part_ref[...] = jnp.broadcast_to(both[None], (copies, 2, LANES))
-    loads[2].wait()
+    loads[3].wait()
     odd_x, odd_y, odd_z = odd("gx_1"), odd("gy_1"), odd("gz")
     for n, ref in enumerate((dens_ref, mom_ref, fuel_ref)):
         low, high = ref[0:half], ref[size_x - half : size_x]
@@ -104,8 +108,8 @@
         xb_ref[n] = jnp.where(odd_x, high, low)
     for n, ref in enumerate((mom_ref, fuel_ref)):
         low, high = ref[:, 0:half, :], ref[:, size_y - half : size_y, :]
-        ya_ref[n] = jnp.where(odd_y, low, high)
-        yb_ref[n] = jnp.where(odd_y, high, low)
+        sides_ref[n * size_x : (n + 1) * size_x] = jnp.where(odd_y, low, high)
+        sides_ref[(n + 2) * size_x : (n + 3) * size_x] = jnp.where(odd_y, high, low)
     turned = [ref[...].reshape(rows, size_z).T for ref in (mom_ref, fuel_ref)]
     low = jnp.concatenate([t[0:half] for t in turned], axis=0)
     high = jnp.concatenate([t[size_z - half : size_z] for t in turned], axis=0)
@@ -123,17 +127,20 @@
         (size_z, 2 * LANES),
         (3, 4, size_y, size_z),
         (3, 4, size_y, size_z),
-        (2, size_x, 4, size_z),
-        (2, size_x, 4, size_z),
+        (4 * size_x, 4, size_z),
         (8, size_x * size_y),
         (8, size_x * size_y),
+    )
+    density, momentum, hydrogen, modes = (
+        pltpu.with_memory_space_constraint(f, pltpu.HBM) for f in (density, momentum, hydrogen, modes)
     )
     return pl.pallas_call(
         functools.partial(partial_kernel, full, copies),
         out_shape=[jax.ShapeDtypeStruct(s, f32) for s in shapes],
-        in_specs=[pl.BlockSpec(memory_space=pltpu.HBM)] * 3 + [VMEM],
+        in_specs=[pl.BlockSpec(memory_space=pltpu.HBM)] * 4,
         out_specs=[VMEM] * len(shapes),
-        scratch_shapes=[pltpu.VMEM(density.shape, f32)] * 3 + [pltpu.SemaphoreType.DMA((3,))],
+        scratch_shapes=[pltpu.VMEM(density.shape, f32)] * 3
+        + [pltpu.VMEM(modes.shape, modes.dtype), pltpu.SemaphoreType.DMA((4,))],
         compiler_params=pltpu.CompilerParams(vmem_limit_bytes=16 << 20),
         name="partial_sums",
     )(density, momentum, hydrogen, modes)
@@ -154,6 +161,24 @@
     )(parts)
 
 
+def pack_kernel(sides_ref, depth_ref, out_ref):
+    count = sides_ref.shape[0]
+    out_ref[0:count] = sides_ref[...]
+    out_ref[count] = depth_ref[0:4]
+    out_ref[count + 1] = depth_ref[4:8]
+
+
+def packed(sides, depth):
+    return pl.pallas_call(
+        pack_kernel,
+        out_shape=jax.ShapeDtypeStruct((sides.shape[0] + 2,) + sides.shape[1:], jnp.float32),
+        in_specs=[VMEM] * 2,
+        out_specs=VMEM,
+        compiler_params=pltpu.CompilerParams(vmem_limit_bytes=4 << 20),
+        name="packed",
+    )(sides, depth)
+
+
 def first_diff(planes, at):
     total = None
     for offset, weight in enumerate(FIRST_COEFFS, 1):
@@ -171,7 +196,7 @@
 
 def final_kernel(
     ncell, dens_ref, mom_ref, fuel_ref, summed_ref, cos_ref, sin_ref, depth_ref,
-    xa_ref, xb_ref, ya_ref, yb_ref, za_ref, zb_ref,
+    xa_ref, xb_ref, traded_ref, relayed_ref, za_ref, zb_ref,
     dens_out, mom_out, fuel_out, force_ref,
 ):
     size_x, size_y, size_z = mom_ref.shape
@@ -191,8 +216,13 @@
     ).reshape(size_x, size_y, size_z)
     gap = jnp.zeros((56, rows), jnp.float32)
     odd_x, odd_y, odd_z = odd("gx_1"), odd("gy_1"), odd("gz")
-    before = jnp.where(odd_z, za_ref[...], zb_ref[...])
-    after = jnp.where(odd_z, zb_ref[...], za_ref[...])
+    place = lax.axis_index("gz")
+    at_end = jnp.logical_or(place == 0, place == lax.axis_size("gz") - 1)
+    za, zb = za_ref[...], zb_ref[...]
+    swapped = jnp.concatenate([traded_ref[4 * size_x], traded_ref[4 * size_x + 1]], axis=0)
+    zb = jnp.where(at_end, swapped, zb)
+    before = jnp.where(odd_z, za, zb)
+    after = jnp.where(odd_z, zb, za)
     turned = jnp.concatenate(
         [after[0:4], gap, before[4:8], after[4:8], gap, before[0:4]], axis=0
     ).T
@@ -213,7 +243,7 @@
         spread = []
         for n, planes in enumerate((mom, fuel)):
             here = planes[at]
-            ya, yb = ya_ref[n, i], yb_ref[n, i]
+            ya, yb = traded_ref[n * size_x + i], relayed_ref[n * size_x + i]
             tall = jnp.concatenate([jnp.where(odd_y, ya, yb), here, jnp.where(odd_y, yb, ya)], axis=0)
             edge = halo[n][i * size_y : (i + 1) * size_y]
 
@@ -255,6 +285,13 @@
     return lax.ppermute(x, axes, pairs + [(j, i) for i, j in pairs])
 
 
+def relay(x):
+    size = lax.axis_size("gy_0")
+    ups = [(2 * i, 2 * ((i + 1) % size)) for i in range(size)]
+    downs = [(2 * i + 1, 2 * ((i - 1) % size) + 1) for i in range(size)]
+    return lax.ppermute(x, GY, ups + downs)
+
+
 def exchange(x, axes):
     return lax.all_to_all(x, axes, 0, 0, tiled=True)
 
@@ -267,18 +304,20 @@
         size_z * lax.axis_size(GZ),
     )
     first, second = lax.axis_size(FIRST_GROUP), lax.axis_size(SECOND_GROUP)
-    part, cos, sin, depth, xa, xb, ya, yb, za, zb = partial_sums(
+    part, cos, sin, depth, xa, xb, sides, za, zb = partial_sums(
         density, momentum, hydrogen, forced_modes.T, full, first
     )
+    za, zb = swap(za, RING, 0), swap(zb, RING, 1)
     part = exchange(part, FIRST_GROUP)
-    ya, yb = swap(ya, GY, 0), swap(yb, GY, 1)
+    sides = packed(sides, zb)
+    traded = swap(sides, ("gy_1",), 0)
     part = summed_copies(part, second)
     part = exchange(part, SECOND_GROUP)
     xa, xb = swap(xa, GX, 0), swap(xb, GX, 1)
-    za, zb = swap(za, GZ, 0), swap(zb, GZ, 1)
+    relayed = relay(traded[2 * size_x : 4 * size_x])
     rates = final_rates(
-        density, momentum, hydrogen, part, cos, sin, depth, (xa, xb, ya, yb, za, zb),
-        float(full[0] * full[1] * full[2]),
+        density, momentum, hydrogen, part, cos, sin, depth,
+        (xa, xb, traded, relayed, za, zb), float(full[0] * full[1] * full[2]),
     )
     return tuple(rates)
 

time: 83.5 us -> 75.1 us (0.90)
  the two profiles are of different devices: /device:TPU:8 before, /device:TPU:6 now
where the time goes in v3:
time: 75.1 us; the launch traced here: 74.6 us
  starting transfers between devices  41.2 us (55%)
  blocking collectives  24 us (32%)
  waiting for transfers between devices  5.37 us (7%)
  Pallas kernels  3.32 us (4%)
  between operations  0.76 us (1%)
    all_to_all x1, blocking collectives, exchange(): return lax.all_to_all(x, axes, 0, 0, tiled=True)  24 us
    ppermute x5, starting transfers between devices, swap(): return lax.ppermute(x, axes, pairs + [(j, i) for i, j in pairs])  23.8 us
    all_to_all x1, starting transfers between devices, exchange(): return lax.all_to_all(x, axes, 0, 0, tiled=True)  13.3 us
    ppermute x5, waiting for transfers between devices, swap(): return lax.ppermute(x, axes, pairs + [(j, i) for i, j in pairs])  5.37 us
    ppermute x1, starting transfers between devices, relay(): return lax.ppermute(x, GY, ups + downs)  4.08 us
  transfers between devices with their start and end apart: 7, of which 2 were waited for; matrix products, arithmetic and copies ran while one was open for 0% of the time, Pallas kernels for 0%

profile of v3, /device:TPU:6, one launch (start us, length us, event | category | flops | bytes accessed | tf_op | source)
XLA Modules:
  0.0 74.6 jit_solution(15125293617619449960)
XLA Ops:
  0.6 1.3 %partial_sums.1 = (f32[32,2,128]{2,1,0:T(2,128)S(1)}, f32[8,16,128]{2,1,0:T(8,128)S(1)}, f32[8,16,128]{2,1,0:T(8,128)S(1)}, f32[128,256]{1,0:T(8,128)S(1)}, f32[...) custom-call(f32[8,16,128]{2,1,0:T(8,128)} %dens_ref.1, ...), custom_call_target="tpu_custom_call" | custom-call | tf_op jit(solution)/shard_map/partial_sums/pallas_call | solution.py:137
  2.0 24.0 %all_to_all.10.parts_ref = f32[32,2,128]{2,1,0:T(2,128)S(1)} all-to-all(f32[32,2,128]{2,1,0:T(2,128)S(1)} %get-tuple-element.12), channel_id=1, replica_groups=mesh['gx_0'=8,'gx_1'=2,'gy_0'=4,'gy_1'=2,'gz'=8] {'gx_0','gy_0'}, dimensions={0} | all-to-all | bytes 65536 | tf_op jit(solution)/shard_map/all_to_all | solution.py:296
  25.9 0.7 summed_copies.1
  26.6 13.3 %all-to-all-start.1 = ((f32[32,2,128]{2,1,0:T(2,128)}), f32[32,2,128]{2,1,0:T(2,128)S(1)}, u32[]{:S(2)}, u32[]{:S(2)}) async-start(f32[32,2,128]{2,1,0:T(2,128)} %summed_copies.1), calls=%async_computation.1 | async-start | bytes 65536 | tf_op jit(solution)/shard_map/all_to_all | solution.py:296
  39.9 4.9 %collective-permute-start.2 = (f32[8,128]{1,0:T(8,128)S(1)}, f32[8,128]{1,0:T(8,128)S(1)}, u32[]{:S(2)}, u32[]{:S(2)}) collective-permute-start(f32[8,128]{1,0:T(8,128)S(1)} %get-tuple-element.19), channel_id=1, source_target_pairs={{1,2},{3,4},{5,6},{7,8},{9,10},{11,12},{13,14},{15,0},{2,1},{4,3},... | collective-permute-start | bytes 12296 | tf_op jit(solution)/shard_map/ppermute | solution.py:285
  44.8 1.8 %collective-permute-done.2.depth_ref.zb_ref = f32[8,128]{1,0:T(8,128)S(1)} collective-permute-done((f32[8,128]{1,0:T(8,128)S(1)}, f32[8,128]{1,0:T(8,128)S(1)}, u32[]{:S(2)}, u32[]{:S(2)}) %collective-permute-start.2) | collective-permute-done | bytes 4128 | tf_op jit(solution)/shard_map/ppermute | solution.py:285
  46.6 0.0 copy-start.1
  46.6 0.0 copy-start.2
  46.6 0.0 copy-start
  46.7 12.5 %collective-permute-start.3 = (f32[34,4,128]{2,1,0:T(4,128)S(1)}, f32[34,4,128]{2,1,0:T(4,128)S(1)}, u32[]{:S(2)}, u32[]{:S(2)}) collective-permute-start(f32[34,4,128]{2,1,0:T(4,128)S(1)} %packed.1), channel_id=1, source_target_pairs={{0,8},{8,0},{1,9},{9,1},{2,10},{10,2},{3,11},{11,3},{4,12},{12,4},... | collective-permute-start | bytes 208904 | tf_op jit(solution)/shard_map/ppermute | solution.py:285
  59.2 1.9 %collective-permute-start = (f32[3,4,16,128]{3,2,1,0:T(8,128)S(1)}, f32[3,4,16,128]{3,2,1,0:T(8,128)S(1)}, u32[]{:S(2)}, u32[]{:S(2)}) collective-permute-start(f32[3,4,16,128]{3,2,1,0:T(8,128)S(1)} %get-tuple-element.16), channel_id=1, source_target_pairs={{0,64},{128,192},{256,320},{384,448},{512,576},{640,704},{768,832}... | collective-permute-start | bytes 294920 | tf_op jit(solution)/shard_map/ppermute | solution.py:285
  61.1 2.5 %collective-permute-start.1 = (f32[3,4,16,128]{3,2,1,0:T(8,128)S(1)}, f32[3,4,16,128]{3,2,1,0:T(8,128)S(1)}, u32[]{:S(2)}, u32[]{:S(2)}) collective-permute-start(f32[3,4,16,128]{3,2,1,0:T(8,128)S(1)} %get-tuple-element.17), channel_id=1, source_target_pairs={{64,128},{192,256},{320,384},{448,512},{576,640},{704,768},{832,89... | collective-permute-start | bytes 294920 | tf_op jit(solution)/shard_map/ppermute | solution.py:285
  63.6 0.0 collective-permute-done.3.traded_ref
  63.6 4.1 %collective-permute-start.4 = (f32[16,4,128]{2,1,0:T(4,128)S(1)}, f32[16,4,128]{2,1,0:T(4,128)S(1)}, u32[]{:S(2)}, u32[]{:S(2)}) collective-permute-start(f32[16,4,128]{2,1,0:T(4,128)S(1)} %slice.4), channel_id=1, source_target_pairs={{0,16},{16,32},{32,48},{48,0},{8,56},{24,8},{40,24},{56,40},{1,17}... | collective-permute-start | bytes 98312 | tf_op jit(solution)/shard_map/ppermute | solution.py:292
  67.7 1.9 %collective-permute-start.5 = (f32[8,128]{1,0:T(8,128)S(1)}, f32[8,128]{1,0:T(8,128)S(1)}, u32[]{:S(2)}, u32[]{:S(2)}) collective-permute-start(f32[8,128]{1,0:T(8,128)S(1)} %get-tuple-element.20), channel_id=1, source_target_pairs={{0,1},{2,3},{4,5},{6,7},{8,9},{10,11},{12,13},{14,15},{1,0},{3,2},... | collective-permute-start | bytes 12296 | tf_op jit(solution)/shard_map/ppermute | solution.py:285
  69.7 3.6 %collective-permute-done.5.za_ref = f32[8,128]{1,0:T(8,128)S(1)} collective-permute-done((f32[8,128]{1,0:T(8,128)S(1)}, f32[8,128]{1,0:T(8,128)S(1)}, u32[]{:S(2)}, u32[]{:S(2)}) %collective-permute-start.5) | collective-permute-done | bytes 4128 | tf_op jit(solution)/shard_map/ppermute | solution.py:285
  73.2 0.0 collective-permute-done.xa_ref
  73.2 0.0 collective-permute-done.1.xb_ref
  73.2 0.0 collective-permute-done.4.relayed_ref
  73.2 0.0 all-to-all-done.1.summed_ref
  73.2 0.0 copy-done.1
  73.3 0.0 copy-done.2
  73.3 0.0 copy-done
  73.3 1.3 %final_rates.1 = (f32[8,16,128]{2,1,0:T(8,128)}, f32[8,16,128]{2,1,0:T(8,128)}, f32[8,16,128]{2,1,0:T(8,128)}) custom-call(f32[8,16,128]{2,1,0:T(8,128)S(1)} %copy-done, f32[8,16,128]{2,1,0:T(8,128)S(1)} %copy-done.1, f32[8,16,128]{2,1,0:T(8,128)S(1)} %copy-done.2, f32[32,2,128]{2,1,0:T(2,128)S(1)} %all-to-all-done.1.summed_ref, ...), custom_call_target="tpu_custom_call" | custom-call | tf_op jit(solution)/shard_map/final_rates/pallas_call | solution.py:271
  (2 shorter events, 0.0 us)
Async XLA Ops:
  26.6 46.7 %all-to-all-start.1 = ((f32[32,2,128]{2,1,0:T(2,128)}), f32[32,2,128]{2,1,0:T(2,128)S(1)}, u32[]{:S(2)}, u32[]{:S(2)}) async-start(f32[32,2,128]{2,1,0:T(2,128)} %summed_copies.1), calls=%async_computation.1 | async-start | bytes 65536 | tf_op jit(solution)/shard_map/all_to_all | solution.py:296
  39.9 6.7 %collective-permute-start.2 = (f32[8,128]{1,0:T(8,128)S(1)}, f32[8,128]{1,0:T(8,128)S(1)}, u32[]{:S(2)}, u32[]{:S(2)}) collective-permute-start(f32[8,128]{1,0:T(8,128)S(1)} %get-tuple-element.19), channel_id=1, source_target_pairs={{1,2},{3,4},{5,6},{7,8},{9,10},{11,12},{13,14},{15,0},{2,1},{4,3},... | collective-permute-start | bytes 12296 | tf_op jit(solution)/shard_map/ppermute | solution.py:285
  46.6 26.6 %copy-start.1 = (f32[8,16,128]{2,1,0:T(8,128)S(1)}, f32[8,16,128]{2,1,0:T(8,128)}, u32[]{:S(2)}) copy-start(f32[8,16,128]{2,1,0:T(8,128)} %mom_ref.1) | copy-start | bytes 196612
  46.6 26.6 %copy-start.2 = (f32[8,16,128]{2,1,0:T(8,128)S(1)}, f32[8,16,128]{2,1,0:T(8,128)}, u32[]{:S(2)}) copy-start(f32[8,16,128]{2,1,0:T(8,128)} %fuel_ref.1) | copy-start | bytes 196612
  46.6 26.6 %copy-start = (f32[8,16,128]{2,1,0:T(8,128)S(1)}, f32[8,16,128]{2,1,0:T(8,128)}, u32[]{:S(2)}) copy-start(f32[8,16,128]{2,1,0:T(8,128)} %dens_ref.1) | copy-start | bytes 196612
  46.7 17.0 %collective-permute-start.3 = (f32[34,4,128]{2,1,0:T(4,128)S(1)}, f32[34,4,128]{2,1,0:T(4,128)S(1)}, u32[]{:S(2)}, u32[]{:S(2)}) collective-permute-start(f32[34,4,128]{2,1,0:T(4,128)S(1)} %packed.1), channel_id=1, source_target_pairs={{0,8},{8,0},{1,9},{9,1},{2,10},{10,2},{3,11},{11,3},{4,12},{12,4},... | collective-permute-start | bytes 208904 | tf_op jit(solution)/shard_map/ppermute | solution.py:285
  59.2 14.0 %collective-permute-start = (f32[3,4,16,128]{3,2,1,0:T(8,128)S(1)}, f32[3,4,16,128]{3,2,1,0:T(8,128)S(1)}, u32[]{:S(2)}, u32[]{:S(2)}) collective-permute-start(f32[3,4,16,128]{3,2,1,0:T(8,128)S(1)} %get-tuple-element.16), channel_id=1, source_target_pairs={{0,64},{128,192},{256,320},{384,448},{512,576},{640,704},{768,832}... | collective-permute-start | bytes 294920 | tf_op jit(solution)/shard_map/ppermute | solution.py:285
  61.1 12.1 %collective-permute-start.1 = (f32[3,4,16,128]{3,2,1,0:T(8,128)S(1)}, f32[3,4,16,128]{3,2,1,0:T(8,128)S(1)}, u32[]{:S(2)}, u32[]{:S(2)}) collective-permute-start(f32[3,4,16,128]{3,2,1,0:T(8,128)S(1)} %get-tuple-element.17), channel_id=1, source_target_pairs={{64,128},{192,256},{320,384},{448,512},{576,640},{704,768},{832,89... | collective-permute-start | bytes 294920 | tf_op jit(solution)/shard_map/ppermute | solution.py:285
  63.6 9.6 %collective-permute-start.4 = (f32[16,4,128]{2,1,0:T(4,128)S(1)}, f32[16,4,128]{2,1,0:T(4,128)S(1)}, u32[]{:S(2)}, u32[]{:S(2)}) collective-permute-start(f32[16,4,128]{2,1,0:T(4,128)S(1)} %slice.4), channel_id=1, source_target_pairs={{0,16},{16,32},{32,48},{48,0},{8,56},{24,8},{40,24},{56,40},{1,17}... | collective-permute-start | bytes 98312 | tf_op jit(solution)/shard_map/ppermute | solution.py:292
  67.7 5.5 %collective-permute-start.5 = (f32[8,128]{1,0:T(8,128)S(1)}, f32[8,128]{1,0:T(8,128)S(1)}, u32[]{:S(2)}, u32[]{:S(2)}) collective-permute-start(f32[8,128]{1,0:T(8,128)S(1)} %get-tuple-element.20), channel_id=1, source_target_pairs={{0,1},{2,3},{4,5},{6,7},{8,9},{10,11},{12,13},{14,15},{1,0},{3,2},... | collective-permute-start | bytes 12296 | tf_op jit(solution)/shard_map/ppermute | solution.py:285

commit v4 on v3

--- a/solution.py
+++ b/solution.py
@@ -12,9 +12,9 @@
 GX = ("gx_0", "gx_1")
 GY = ("gy_0", "gy_1")
 GZ = ("gz",)
-FIRST_GROUP = ("gx_0", "gy_0")
+FIRST_GROUP = ("gx_1", "gy_1", "gz")
 RING = ("gy_1", "gz")
-SECOND_GROUP = ("gx_1", "gy_1", "gz")
+SECOND_GROUP = ("gx_0", "gy_0")
 
 FIRST_COEFFS = (0.8, -0.2, 4.0 / 105.0, -1.0 / 280.0)
 SECOND_COEFFS = (1.6, -0.2, 8.0 / 315.0, -1.0 / 560.0)
@@ -44,7 +44,7 @@
 def partial_kernel(
     full, copies, dens_hbm, mom_hbm, fuel_hbm, modes_hbm,
     part_ref, cos_ref, sin_ref, depth_ref,
-    xa_ref, xb_ref, sides_ref, za_ref, zb_ref,
+    xlo_ref, xhi_ref, sides_ref, za_ref, zb_ref,
     dens_ref, mom_ref, fuel_ref, modes_ref, sems,
 ):
     size_x, size_y, size_z = mom_ref.shape
@@ -101,11 +101,10 @@
     both = jnp.concatenate([part_cos, part_sin], axis=0)
     part_ref[...] = jnp.broadcast_to(both[None], (copies, 2, LANES))
     loads[3].wait()
-    odd_x, odd_y, odd_z = odd("gx_1"), odd("gy_1"), odd("gz")
+    odd_y, odd_z = odd("gy_1"), odd("gz")
     for n, ref in enumerate((dens_ref, mom_ref, fuel_ref)):
-        low, high = ref[0:half], ref[size_x - half : size_x]
-        xa_ref[n] = jnp.where(odd_x, low, high)
-        xb_ref[n] = jnp.where(odd_x, high, low)
+        xlo_ref[n] = ref[0:half]
+        xhi_ref[n] = ref[size_x - half : size_x]
     for n, ref in enumerate((mom_ref, fuel_ref)):
         low, high = ref[:, 0:half, :], ref[:, size_y - half : size_y, :]
         sides_ref[n * size_x : (n + 1) * size_x] = jnp.where(odd_y, low, high)
@@ -196,7 +195,7 @@
 
 def final_kernel(
     ncell, dens_ref, mom_ref, fuel_ref, summed_ref, cos_ref, sin_ref, depth_ref,
-    xa_ref, xb_ref, traded_ref, relayed_ref, za_ref, zb_ref,
+    xbefore_ref, xafter_ref, traded_ref, relayed_ref, za_ref, zb_ref,
     dens_out, mom_out, fuel_out, force_ref,
 ):
     size_x, size_y, size_z = mom_ref.shape
@@ -215,7 +214,7 @@
         preferred_element_type=jnp.float32,
     ).reshape(size_x, size_y, size_z)
     gap = jnp.zeros((56, rows), jnp.float32)
-    odd_x, odd_y, odd_z = odd("gx_1"), odd("gy_1"), odd("gz")
+    odd_y, odd_z = odd("gy_1"), odd("gz")
     place = lax.axis_index("gz")
     at_end = jnp.logical_or(place == 0, place == lax.axis_size("gz") - 1)
     za, zb = za_ref[...], zb_ref[...]
@@ -229,9 +228,7 @@
     halo = [turned, pltpu.roll(turned, 64, 1)]
     lane = lax.broadcasted_iota(jnp.int32, (1, size_z), 1)
     dens, mom, fuel = (
-        [jnp.where(odd_x, xa_ref[n, i], xb_ref[n, i]) for i in range(4)]
-        + [ref[i] for i in range(size_x)]
-        + [jnp.where(odd_x, xb_ref[n, i], xa_ref[n, i]) for i in range(4)]
+        [xbefore_ref[n, i] for i in range(4)] + [ref[i] for i in range(size_x)] + [xafter_ref[n, i] for i in range(4)]
         for n, ref in enumerate((dens_ref, mom_ref, fuel_ref))
     )
     vel = [m / d for m, d in zip(mom, dens)]
@@ -279,6 +276,11 @@
     )(density, momentum, hydrogen, summed, cos, sin, depth, *halos)
 
 
+def shift(x, axes, by):
+    size = lax.axis_size(axes)
+    return lax.ppermute(x, axes, [(i, (i + by) % size) for i in range(size)])
+
+
 def swap(x, axes, shift):
     size = lax.axis_size(axes)
     pairs = [((i + shift) % size, (i + 1 + shift) % size) for i in range(0, size, 2)]
@@ -304,20 +306,21 @@
         size_z * lax.axis_size(GZ),
     )
     first, second = lax.axis_size(FIRST_GROUP), lax.axis_size(SECOND_GROUP)
-    part, cos, sin, depth, xa, xb, sides, za, zb = partial_sums(
+    part, cos, sin, depth, xlo, xhi, sides, za, zb = partial_sums(
         density, momentum, hydrogen, forced_modes.T, full, first
     )
-    za, zb = swap(za, RING, 0), swap(zb, RING, 1)
+    zb = swap(zb, RING, 1)
     part = exchange(part, FIRST_GROUP)
     sides = packed(sides, zb)
     traded = swap(sides, ("gy_1",), 0)
     part = summed_copies(part, second)
     part = exchange(part, SECOND_GROUP)
-    xa, xb = swap(xa, GX, 0), swap(xb, GX, 1)
+    xbefore, xafter = shift(xhi, GX, 1), shift(xlo, GX, -1)
+    za = swap(za, GZ, 0)
     relayed = relay(traded[2 * size_x : 4 * size_x])
     rates = final_rates(
         density, momentum, hydrogen, part, cos, sin, depth,
-        (xa, xb, traded, relayed, za, zb), float(full[0] * full[1] * full[2]),
+        (xbefore, xafter, traded, relayed, za, zb), float(full[0] * full[1] * full[2]),
     )
     return tuple(rates)
 

time: 75.1 us -> 65.5 us (0.87)
  the two profiles are of different devices: /device:TPU:6 before, /device:TPU:2 now
where the time goes in v4:
time: 65.5 us; the launch traced here: 65.1 us
  starting transfers between devices  55.1 us (84%)
  waiting for transfers between devices  5.38 us (8%)
  Pallas kernels  3.84 us (6%)
  between operations  0.75 us (1%)
    all_to_all x2, starting transfers between devices, exchange(): return lax.all_to_all(x, axes, 0, 0, tiled=True)  29.5 us
    ppermute x3, starting transfers between devices, swap(): return lax.ppermute(x, axes, pairs + [(j, i) for i, j in pairs])  19.2 us
    ppermute x3, waiting for transfers between devices, swap(): return lax.ppermute(x, axes, pairs + [(j, i) for i, j in pairs])  5.36 us
    ppermute x1, starting transfers between devices, relay(): return lax.ppermute(x, GY, ups + downs)  3.37 us
    ppermute x2, starting transfers between devices, shift(): return lax.ppermute(x, axes, [(i, (i + by) % size) for i in range(size)])  2.96 us
    pallas_call x1, Pallas kernels, partial_sums(): pl.pallas_call(functools.partial(partial_kernel, full, copies), out_shape...  1.84 us
    pallas_call x1, Pallas kernels, final_rates(): pl.pallas_call(functools.partial(final_kernel, ncell), out_shape=[jax.Sha...  1.34 us
  transfers between devices with their start and end apart: 8, of which 2 were waited for; matrix products, arithmetic and copies ran while one was open for 0% of the time, Pallas kernels for 1%

profile of v4, /device:TPU:2, one launch (start us, length us, event | category | flops | bytes accessed | tf_op | source)
XLA Modules:
  0.0 65.1 jit_solution(14480944554255250512)
XLA Ops:
  0.6 1.8 %partial_sums.1 = (f32[32,2,128]{2,1,0:T(2,128)}, f32[8,16,128]{2,1,0:T(8,128)S(1)}, f32[8,16,128]{2,1,0:T(8,128)S(1)}, f32[128,256]{1,0:T(8,128)S(1)}, f32[3,4,...) custom-call(f32[8,16,128]{2,1,0:T(8,128)} %dens_ref.1, ...), custom_call_target="tpu_custom_call" | custom-call | tf_op jit(solution)/shard_map/partial_sums/pallas_call | solution.py:136
  2.5 19.2 %all-to-all-start = ((f32[32,2,128]{2,1,0:T(2,128)}), f32[32,2,128]{2,1,0:T(2,128)S(1)}, u32[]{:S(2)}, u32[]{:S(2)}) async-start(f32[32,2,128]{2,1,0:T(2,128)} %get-tuple-element.12), calls=%async_computation | async-start | bytes 65536 | tf_op jit(solution)/shard_map/all_to_all | solution.py:298
  21.7 4.9 %collective-permute-start.2 = (f32[8,128]{1,0:T(8,128)S(1)}, f32[8,128]{1,0:T(8,128)S(1)}, u32[]{:S(2)}, u32[]{:S(2)}) collective-permute-start(f32[8,128]{1,0:T(8,128)S(1)} %get-tuple-element.19), channel_id=1, source_target_pairs={{1,2},{3,4},{5,6},{7,8},{9,10},{11,12},{13,14},{15,0},{2,1},{4,3},... | collective-permute-start | bytes 12296 | tf_op jit(solution)/shard_map/ppermute | solution.py:287
  26.6 1.8 %collective-permute-done.2.depth_ref.zb_ref = f32[8,128]{1,0:T(8,128)S(1)} collective-permute-done((f32[8,128]{1,0:T(8,128)S(1)}, f32[8,128]{1,0:T(8,128)S(1)}, u32[]{:S(2)}, u32[]{:S(2)}) %collective-permute-start.2) | collective-permute-done | bytes 4128 | tf_op jit(solution)/shard_map/ppermute | solution.py:287
  28.4 12.4 %collective-permute-start.3 = (f32[34,4,128]{2,1,0:T(4,128)S(1)}, f32[34,4,128]{2,1,0:T(4,128)S(1)}, u32[]{:S(2)}, u32[]{:S(2)}) collective-permute-start(f32[34,4,128]{2,1,0:T(4,128)S(1)} %packed.1), channel_id=1, source_target_pairs={{0,8},{8,0},{1,9},{9,1},{2,10},{10,2},{3,11},{11,3},{4,12},{12,4},... | collective-permute-start | bytes 208904 | tf_op jit(solution)/shard_map/ppermute | solution.py:287
  40.8 0.0 collective-permute-start
  40.8 2.9 %collective-permute-start.1 = (f32[3,4,16,128]{3,2,1,0:T(8,128)S(1)}, f32[3,4,16,128]{3,2,1,0:T(8,128)S(1)}, u32[]{:S(2)}, u32[]{:S(2)}) collective-permute-start(f32[3,4,16,128]{3,2,1,0:T(8,128)S(1)} %get-tuple-element.17), channel_id=1, source_target_pairs={{0,960},{64,0},{128,64},{192,128},{256,192},{320,256},{384,320},{4... | collective-permute-start | bytes 294920 | tf_op jit(solution)/shard_map/ppermute | solution.py:281
  43.8 0.0 all-to-all-done.parts_ref
  43.8 0.0 copy-start.2
  43.8 0.7 %summed_copies.1 = f32[32,2,128]{2,1,0:T(2,128)} custom-call(f32[32,2,128]{2,1,0:T(2,128)S(1)} %all-to-all-done.parts_ref), custom_call_target="tpu_custom_call" | custom-call | tf_op jit(solution)/shard_map/summed_copies/pallas_call | solution.py:153
  44.4 0.0 copy-start
  44.4 0.0 copy-start.1
  44.4 10.4 %all-to-all-start.1 = ((f32[32,2,128]{2,1,0:T(2,128)}), f32[32,2,128]{2,1,0:T(2,128)S(1)}, u32[]{:S(2)}, u32[]{:S(2)}) async-start(f32[32,2,128]{2,1,0:T(2,128)} %summed_copies.1), calls=%async_computation.1 | async-start | bytes 65536 | tf_op jit(solution)/shard_map/all_to_all | solution.py:298
  54.8 0.0 collective-permute-done.3.traded_ref
  54.8 3.4 %collective-permute-start.4 = (f32[16,4,128]{2,1,0:T(4,128)S(1)}, f32[16,4,128]{2,1,0:T(4,128)S(1)}, u32[]{:S(2)}, u32[]{:S(2)}) collective-permute-start(f32[16,4,128]{2,1,0:T(4,128)S(1)} %slice.4), channel_id=1, source_target_pairs={{0,16},{16,32},{32,48},{48,0},{8,56},{24,8},{40,24},{56,40},{1,17}... | collective-permute-start | bytes 98312 | tf_op jit(solution)/shard_map/ppermute | solution.py:294
  58.2 1.9 %collective-permute-start.5 = (f32[8,128]{1,0:T(8,128)S(1)}, f32[8,128]{1,0:T(8,128)S(1)}, u32[]{:S(2)}, u32[]{:S(2)}) collective-permute-start(f32[8,128]{1,0:T(8,128)S(1)} %get-tuple-element.20), channel_id=1, source_target_pairs={{0,1},{2,3},{4,5},{6,7},{1,0},{3,2},{5,4},{7,6},{8,9},{10,11},{12,... | collective-permute-start | bytes 12296 | tf_op jit(solution)/shard_map/ppermute | solution.py:287
  60.1 3.6 %collective-permute-done.5.za_ref = f32[8,128]{1,0:T(8,128)S(1)} collective-permute-done((f32[8,128]{1,0:T(8,128)S(1)}, f32[8,128]{1,0:T(8,128)S(1)}, u32[]{:S(2)}, u32[]{:S(2)}) %collective-permute-start.5) | collective-permute-done | bytes 4128 | tf_op jit(solution)/shard_map/ppermute | solution.py:287
  63.7 0.0 collective-permute-done.xbefore_ref
  63.7 0.0 collective-permute-done.1.xafter_ref
  63.7 0.0 collective-permute-done.4.relayed_ref
  63.7 0.0 all-to-all-done.1.summed_ref
  63.7 0.0 copy-done.2
  63.7 0.0 copy-done
  63.8 0.0 copy-done.1
  63.8 1.3 %final_rates.1 = (f32[8,16,128]{2,1,0:T(8,128)}, f32[8,16,128]{2,1,0:T(8,128)}, f32[8,16,128]{2,1,0:T(8,128)}) custom-call(f32[8,16,128]{2,1,0:T(8,128)S(1)} %copy-done, f32[8,16,128]{2,1,0:T(8,128)S(1)} %copy-done.1, f32[8,16,128]{2,1,0:T(8,128)S(1)} %copy-done.2, f32[32,2,128]{2,1,0:T(2,128)S(1)} %all-to-all-done.1.summed_ref, ...), custom_call_target="tpu_custom_call" | custom-call | tf_op jit(solution)/shard_map/final_rates/pallas_call | solution.py:268
  (2 shorter events, 0.0 us)
Async XLA Ops:
  2.5 41.3 %all-to-all-start = ((f32[32,2,128]{2,1,0:T(2,128)}), f32[32,2,128]{2,1,0:T(2,128)S(1)}, u32[]{:S(2)}, u32[]{:S(2)}) async-start(f32[32,2,128]{2,1,0:T(2,128)} %get-tuple-element.12), calls=%async_computation | async-start | bytes 65536 | tf_op jit(solution)/shard_map/all_to_all | solution.py:298
  21.7 6.7 %collective-permute-start.2 = (f32[8,128]{1,0:T(8,128)S(1)}, f32[8,128]{1,0:T(8,128)S(1)}, u32[]{:S(2)}, u32[]{:S(2)}) collective-permute-start(f32[8,128]{1,0:T(8,128)S(1)} %get-tuple-element.19), channel_id=1, source_target_pairs={{1,2},{3,4},{5,6},{7,8},{9,10},{11,12},{13,14},{15,0},{2,1},{4,3},... | collective-permute-start | bytes 12296 | tf_op jit(solution)/shard_map/ppermute | solution.py:287
  28.4 26.4 %collective-permute-start.3 = (f32[34,4,128]{2,1,0:T(4,128)S(1)}, f32[34,4,128]{2,1,0:T(4,128)S(1)}, u32[]{:S(2)}, u32[]{:S(2)}) collective-permute-start(f32[34,4,128]{2,1,0:T(4,128)S(1)} %packed.1), channel_id=1, source_target_pairs={{0,8},{8,0},{1,9},{9,1},{2,10},{10,2},{3,11},{11,3},{4,12},{12,4},... | collective-permute-start | bytes 208904 | tf_op jit(solution)/shard_map/ppermute | solution.py:287
  40.8 22.9 %collective-permute-start = (f32[3,4,16,128]{3,2,1,0:T(8,128)S(1)}, f32[3,4,16,128]{3,2,1,0:T(8,128)S(1)}, u32[]{:S(2)}, u32[]{:S(2)}) collective-permute-start(f32[3,4,16,128]{3,2,1,0:T(8,128)S(1)} %get-tuple-element.16), channel_id=1, source_target_pairs={{0,64},{64,128},{128,192},{192,256},{256,320},{320,384},{384,448},... | collective-permute-start | bytes 294920 | tf_op jit(solution)/shard_map/ppermute | solution.py:281
  40.8 22.9 %collective-permute-start.1 = (f32[3,4,16,128]{3,2,1,0:T(8,128)S(1)}, f32[3,4,16,128]{3,2,1,0:T(8,128)S(1)}, u32[]{:S(2)}, u32[]{:S(2)}) collective-permute-start(f32[3,4,16,128]{3,2,1,0:T(8,128)S(1)} %get-tuple-element.17), channel_id=1, source_target_pairs={{0,960},{64,0},{128,64},{192,128},{256,192},{320,256},{384,320},{4... | collective-permute-start | bytes 294920 | tf_op jit(solution)/shard_map/ppermute | solution.py:281
  43.8 20.0 %copy-start.2 = (f32[8,16,128]{2,1,0:T(8,128)S(1)}, f32[8,16,128]{2,1,0:T(8,128)}, u32[]{:S(2)}) copy-start(f32[8,16,128]{2,1,0:T(8,128)} %fuel_ref.1) | copy-start | bytes 196612
  44.4 19.3 %copy-start = (f32[8,16,128]{2,1,0:T(8,128)S(1)}, f32[8,16,128]{2,1,0:T(8,128)}, u32[]{:S(2)}) copy-start(f32[8,16,128]{2,1,0:T(8,128)} %dens_ref.1) | copy-start | bytes 196612
  44.4 19.3 %copy-start.1 = (f32[8,16,128]{2,1,0:T(8,128)S(1)}, f32[8,16,128]{2,1,0:T(8,128)}, u32[]{:S(2)}) copy-start(f32[8,16,128]{2,1,0:T(8,128)} %mom_ref.1) | copy-start | bytes 196612
  44.4 19.3 %all-to-all-start.1 = ((f32[32,2,128]{2,1,0:T(2,128)}), f32[32,2,128]{2,1,0:T(2,128)S(1)}, u32[]{:S(2)}, u32[]{:S(2)}) async-start(f32[32,2,128]{2,1,0:T(2,128)} %summed_copies.1), calls=%async_computation.1 | async-start | bytes 65536 | tf_op jit(solution)/shard_map/all_to_all | solution.py:298
  54.8 8.9 %collective-permute-start.4 = (f32[16,4,128]{2,1,0:T(4,128)S(1)}, f32[16,4,128]{2,1,0:T(4,128)S(1)}, u32[]{:S(2)}, u32[]{:S(2)}) collective-permute-start(f32[16,4,128]{2,1,0:T(4,128)S(1)} %slice.4), channel_id=1, source_target_pairs={{0,16},{16,32},{32,48},{48,0},{8,56},{24,8},{40,24},{56,40},{1,17}... | collective-permute-start | bytes 98312 | tf_op jit(solution)/shard_map/ppermute | solution.py:294
  58.2 5.5 %collective-permute-start.5 = (f32[8,128]{1,0:T(8,128)S(1)}, f32[8,128]{1,0:T(8,128)S(1)}, u32[]{:S(2)}, u32[]{:S(2)}) collective-permute-start(f32[8,128]{1,0:T(8,128)S(1)} %get-tuple-element.20), channel_id=1, source_target_pairs={{0,1},{2,3},{4,5},{6,7},{1,0},{3,2},{5,4},{7,6},{8,9},{10,11},{12,... | collective-permute-start | bytes 12296 | tf_op jit(solution)/shard_map/ppermute | solution.py:287

commit v5 on v4

--- a/solution.py
+++ b/solution.py
@@ -12,9 +12,9 @@
 GX = ("gx_0", "gx_1")
 GY = ("gy_0", "gy_1")
 GZ = ("gz",)
-FIRST_GROUP = ("gx_1", "gy_1", "gz")
+FIRST_GROUP = ("gx_0", "gy_0")
 RING = ("gy_1", "gz")
-SECOND_GROUP = ("gx_0", "gy_0")
+SECOND_GROUP = ("gx_1", "gy_1", "gz")
 
 FIRST_COEFFS = (0.8, -0.2, 4.0 / 105.0, -1.0 / 280.0)
 SECOND_COEFFS = (1.6, -0.2, 8.0 / 315.0, -1.0 / 560.0)
@@ -113,7 +113,10 @@
     low = jnp.concatenate([t[0:half] for t in turned], axis=0)
     high = jnp.concatenate([t[size_z - half : size_z] for t in turned], axis=0)
     za_ref[...] = jnp.where(odd_z, low, high)
-    zb_ref[...] = jnp.where(odd_z, high, low)
+    edge = jnp.where(odd_z, high, low)
+    zb_ref[...] = edge
+    sides_ref[4 * size_x] = edge[0:4]
+    sides_ref[4 * size_x + 1] = edge[4:8]
 
 
 def partial_sums(density, momentum, hydrogen, modes, full, copies):
@@ -126,7 +129,7 @@
         (size_z, 2 * LANES),
         (3, 4, size_y, size_z),
         (3, 4, size_y, size_z),
-        (4 * size_x, 4, size_z),
+        (4 * size_x + 2, 4, size_z),
         (8, size_x * size_y),
         (8, size_x * size_y),
     )
@@ -160,22 +163,28 @@
     )(parts)
 
 
-def pack_kernel(sides_ref, depth_ref, out_ref):
-    count = sides_ref.shape[0]
-    out_ref[0:count] = sides_ref[...]
-    out_ref[count] = depth_ref[0:4]
-    out_ref[count + 1] = depth_ref[4:8]
-
-
-def packed(sides, depth):
+def forward_kernel(traded_ref, edge_ref, relay_ref, hop_ref):
+    count = relay_ref.shape[0]
+    relay_ref[...] = traded_ref[count : 2 * count]
+    place = lax.axis_index("gz")
+    at_end = jnp.logical_or(place == 0, place == lax.axis_size("gz") - 1)
+    partners = jnp.concatenate([traded_ref[2 * count], traded_ref[2 * count + 1]], axis=0)
+    hop_ref[...] = jnp.where(at_end, partners, edge_ref[...])
+
+
+def forwarded(traded, edge):
+    count = (traded.shape[0] - 2) // 2
     return pl.pallas_call(
-        pack_kernel,
-        out_shape=jax.ShapeDtypeStruct((sides.shape[0] + 2,) + sides.shape[1:], jnp.float32),
+        forward_kernel,
+        out_shape=[
+            jax.ShapeDtypeStruct((count,) + traded.shape[1:], jnp.float32),
+            jax.ShapeDtypeStruct(edge.shape, jnp.float32),
+        ],
         in_specs=[VMEM] * 2,
-        out_specs=VMEM,
+        out_specs=[VMEM] * 2,
         compiler_params=pltpu.CompilerParams(vmem_limit_bytes=4 << 20),
-        name="packed",
-    )(sides, depth)
+        name="forwarded",
+    )(traded, edge)
 
 
 def first_diff(planes, at):
@@ -215,11 +224,7 @@
     ).reshape(size_x, size_y, size_z)
     gap = jnp.zeros((56, rows), jnp.float32)
     odd_y, odd_z = odd("gy_1"), odd("gz")
-    place = lax.axis_index("gz")
-    at_end = jnp.logical_or(place == 0, place == lax.axis_size("gz") - 1)
     za, zb = za_ref[...], zb_ref[...]
-    swapped = jnp.concatenate([traded_ref[4 * size_x], traded_ref[4 * size_x + 1]], axis=0)
-    zb = jnp.where(at_end, swapped, zb)
     before = jnp.where(odd_z, za, zb)
     after = jnp.where(odd_z, zb, za)
     turned = jnp.concatenate(
@@ -309,15 +314,15 @@
     part, cos, sin, depth, xlo, xhi, sides, za, zb = partial_sums(
         density, momentum, hydrogen, forced_modes.T, full, first
     )
-    zb = swap(zb, RING, 1)
+    traded = swap(sides, ("gy_1",), 0)
     part = exchange(part, FIRST_GROUP)
-    sides = packed(sides, zb)
-    traded = swap(sides, ("gy_1",), 0)
+    xbefore, xafter = shift(xhi, GX, 1), shift(xlo, GX, -1)
+    za = swap(za, GZ, 0)
     part = summed_copies(part, second)
     part = exchange(part, SECOND_GROUP)
-    xbefore, xafter = shift(xhi, GX, 1), shift(xlo, GX, -1)
-    za = swap(za, GZ, 0)
-    relayed = relay(traded[2 * size_x : 4 * size_x])
+    relayed, zb = forwarded(traded, zb)
+    relayed = relay(relayed)
+    zb = swap(zb, RING, 1)
     rates = final_rates(
         density, momentum, hydrogen, part, cos, sin, depth,
         (xbefore, xafter, traded, relayed, za, zb), float(full[0] * full[1] * full[2]),

time: 65.5 us -> 72.2 us (1.10)
  blocking collectives: 0 us -> 24.5 us
  starting transfers between devices: 55.1 us -> 39.6 us
  waiting for transfers between devices: 5.38 us -> 3.66 us
    all_to_all x0 -> x1, blocking collectives: none -> 24.5 us  [exchange(): return lax.all_to_all(x, axes, 0, 0, tiled=True)]
    all_to_all x2 -> x1, starting transfers between devices: 29.5 us -> 13.5 us  [exchange(): return lax.all_to_all(x, axes, 0, 0, tiled=True)]
    ppermute x3, waiting for transfers between devices: 5.36 us -> 3.65 us  [swap(): return lax.ppermute(x, axes, pairs + [(j, i) for i, j in pairs])]
    ppermute x3, starting transfers between devices: 19.2 us -> 20.6 us  [swap(): return lax.ppermute(x, axes, pairs + [(j, i) for i, j in pairs])]
    ppermute x1, starting transfers between devices: 3.37 us -> 2.57 us  [relay(): return lax.ppermute(x, GY, ups + downs)]
  transfers between devices with their start and end apart: 8 -> 7, of which waited for: 2 -> 2; matrix products, arithmetic and copies ran while one was open for 0% -> 0% of each run, Pallas kernels for 1% -> 0%
where the time goes in v5:
time: 72.2 us; the launch traced here: 71.8 us
  starting transfers between devices  39.6 us (55%)
  blocking collectives  24.5 us (34%)
  waiting for transfers between devices  3.66 us (5%)
  Pallas kernels  3.33 us (5%)
  between operations  0.73 us (1%)
    all_to_all x1, blocking collectives, exchange(): return lax.all_to_all(x, axes, 0, 0, tiled=True)  24.5 us
    ppermute x3, starting transfers between devices, swap(): return lax.ppermute(x, axes, pairs + [(j, i) for i, j in pairs])  20.6 us
    all_to_all x1, starting transfers between devices, exchange(): return lax.all_to_all(x, axes, 0, 0, tiled=True)  13.5 us
    ppermute x3, waiting for transfers between devices, swap(): return lax.ppermute(x, axes, pairs + [(j, i) for i, j in pairs])  3.65 us
    ppermute x2, starting transfers between devices, shift(): return lax.ppermute(x, axes, [(i, (i + by) % size) for i in range(size)])  2.96 us
    ppermute x1, starting transfers between devices, relay(): return lax.ppermute(x, GY, ups + downs)  2.57 us
  transfers between devices with their start and end apart: 7, of which 2 were waited for; matrix products, arithmetic and copies ran while one was open for 0% of the time, Pallas kernels for 0%

profile of v5, /device:TPU:2, one launch (start us, length us, event | category | flops | bytes accessed | tf_op | source)
XLA Modules:
  0.0 71.8 jit_solution(14894139734384131668)
XLA Ops:
  0.6 1.3 %partial_sums.1 = (f32[32,2,128]{2,1,0:T(2,128)S(1)}, f32[8,16,128]{2,1,0:T(8,128)S(1)}, f32[8,16,128]{2,1,0:T(8,128)S(1)}, f32[128,256]{1,0:T(8,128)S(1)}, f32[...) custom-call(f32[8,16,128]{2,1,0:T(8,128)} %dens_ref.1, ...), custom_call_target="tpu_custom_call" | custom-call | tf_op jit(solution)/shard_map/partial_sums/pallas_call | solution.py:139
  1.9 24.5 %all_to_all.10.parts_ref = f32[32,2,128]{2,1,0:T(2,128)S(1)} all-to-all(f32[32,2,128]{2,1,0:T(2,128)S(1)} %get-tuple-element.14), channel_id=1, replica_groups=mesh['gx_0'=8,'gx_1'=2,'gy_0'=4,'gy_1'=2,'gz'=8] {'gx_0','gy_0'}, dimensions={0} | all-to-all | bytes 65536 | tf_op jit(solution)/shard_map/all_to_all | solution.py:303
  26.5 0.0 copy-start.2
  26.5 0.7 summed_copies.1
  27.1 0.0 copy-start
  27.1 0.0 copy-start.1
  27.1 13.5 %all-to-all-start.1 = ((f32[32,2,128]{2,1,0:T(2,128)}), f32[32,2,128]{2,1,0:T(2,128)S(1)}, u32[]{:S(2)}, u32[]{:S(2)}) async-start(f32[32,2,128]{2,1,0:T(2,128)} %summed_copies.1), calls=%async_computation.1 | async-start | bytes 65536 | tf_op jit(solution)/shard_map/all_to_all | solution.py:303
  40.6 12.4 %collective-permute-start.2 = (f32[34,4,128]{2,1,0:T(4,128)S(1)}, f32[34,4,128]{2,1,0:T(4,128)S(1)}, u32[]{:S(2)}, u32[]{:S(2)}) collective-permute-start(f32[34,4,128]{2,1,0:T(4,128)S(1)} %get-tuple-element.20), channel_id=1, source_target_pairs={{0,8},{8,0},{1,9},{9,1},{2,10},{10,2},{3,11},{11,3},{4,12},{12,4},... | collective-permute-start | bytes 208904 | tf_op jit(solution)/shard_map/ppermute | solution.py:292
  53.0 0.0 collective-permute-start
  53.0 2.9 %collective-permute-start.1 = (f32[3,4,16,128]{3,2,1,0:T(8,128)S(1)}, f32[3,4,16,128]{3,2,1,0:T(8,128)S(1)}, u32[]{:S(2)}, u32[]{:S(2)}) collective-permute-start(f32[3,4,16,128]{3,2,1,0:T(8,128)S(1)} %get-tuple-element.19), channel_id=1, source_target_pairs={{0,960},{64,0},{128,64},{192,128},{256,192},{320,256},{384,320},{4... | collective-permute-start | bytes 294920 | tf_op jit(solution)/shard_map/ppermute | solution.py:286
  56.0 2.1 %collective-permute-done.2.traded_ref = f32[34,4,128]{2,1,0:T(4,128)S(1)} collective-permute-done((f32[34,4,128]{2,1,0:T(4,128)S(1)}, f32[34,4,128]{2,1,0:T(4,128)S(1)}, u32[]{:S(2)}, u32[]{:S(2)}) %collective-permute-start.2) | collective-permute-done | bytes 69664 | tf_op jit(solution)/shard_map/ppermute | solution.py:292
  58.1 2.6 %collective-permute-start.3 = (f32[16,4,128]{2,1,0:T(4,128)S(1)}, f32[16,4,128]{2,1,0:T(4,128)S(1)}, u32[]{:S(2)}, u32[]{:S(2)}) collective-permute-start(f32[16,4,128]{2,1,0:T(4,128)S(1)} %get-tuple-element.22), channel_id=1, source_target_pairs={{0,16},{16,32},{32,48},{48,0},{8,56},{24,8},{40,24},{56,40},{1,17}... | collective-permute-start | bytes 98312 | tf_op jit(solution)/shard_map/ppermute | solution.py:299
  60.7 1.9 %collective-permute-start.4 = (f32[8,128]{1,0:T(8,128)S(1)}, f32[8,128]{1,0:T(8,128)S(1)}, u32[]{:S(2)}, u32[]{:S(2)}) collective-permute-start(f32[8,128]{1,0:T(8,128)S(1)} %get-tuple-element.23), channel_id=1, source_target_pairs={{0,1},{2,3},{4,5},{6,7},{1,0},{3,2},{5,4},{7,6},{8,9},{10,11},{12,... | collective-permute-start | bytes 12296 | tf_op jit(solution)/shard_map/ppermute | solution.py:292
  62.6 6.2 %collective-permute-start.5 = (f32[8,128]{1,0:T(8,128)S(1)}, f32[8,128]{1,0:T(8,128)S(1)}, u32[]{:S(2)}, u32[]{:S(2)}) collective-permute-start(f32[8,128]{1,0:T(8,128)S(1)} %get-tuple-element.24), channel_id=1, source_target_pairs={{1,2},{3,4},{5,6},{7,8},{9,10},{11,12},{13,14},{15,0},{2,1},{4,3},... | collective-permute-start | bytes 12296 | tf_op jit(solution)/shard_map/ppermute | solution.py:292
  68.8 0.0 collective-permute-done.4.za_ref
  68.8 1.6 %collective-permute-done.5.zb_ref = f32[8,128]{1,0:T(8,128)S(1)} collective-permute-done((f32[8,128]{1,0:T(8,128)S(1)}, f32[8,128]{1,0:T(8,128)S(1)}, u32[]{:S(2)}, u32[]{:S(2)}) %collective-permute-start.5) | collective-permute-done | bytes 4128 | tf_op jit(solution)/shard_map/ppermute | solution.py:292
  70.4 0.0 collective-permute-done.xbefore_ref
  70.4 0.0 collective-permute-done.1.xafter_ref
  70.4 0.0 collective-permute-done.3.relayed_ref
  70.4 0.0 all-to-all-done.1.summed_ref
  70.4 0.0 copy-done.2
  70.4 0.0 copy-done
  70.4 0.0 copy-done.1
  70.5 1.4 %final_rates.1 = (f32[8,16,128]{2,1,0:T(8,128)}, f32[8,16,128]{2,1,0:T(8,128)}, f32[8,16,128]{2,1,0:T(8,128)}) custom-call(f32[8,16,128]{2,1,0:T(8,128)S(1)} %copy-done, f32[8,16,128]{2,1,0:T(8,128)S(1)} %copy-done.1, f32[8,16,128]{2,1,0:T(8,128)S(1)} %copy-done.2, f32[32,2,128]{2,1,0:T(2,128)S(1)} %all-to-all-done.1.summed_ref, ...), custom_call_target="tpu_custom_call" | custom-call | tf_op jit(solution)/shard_map/final_rates/pallas_call | solution.py:273
  (1 shorter events, 0.0 us)
Async XLA Ops:
  26.5 44.0 %copy-start.2 = (f32[8,16,128]{2,1,0:T(8,128)S(1)}, f32[8,16,128]{2,1,0:T(8,128)}, u32[]{:S(2)}) copy-start(f32[8,16,128]{2,1,0:T(8,128)} %fuel_ref.1) | copy-start | bytes 196612
  27.1 43.3 %copy-start = (f32[8,16,128]{2,1,0:T(8,128)S(1)}, f32[8,16,128]{2,1,0:T(8,128)}, u32[]{:S(2)}) copy-start(f32[8,16,128]{2,1,0:T(8,128)} %dens_ref.1) | copy-start | bytes 196612
  27.1 43.3 %copy-start.1 = (f32[8,16,128]{2,1,0:T(8,128)S(1)}, f32[8,16,128]{2,1,0:T(8,128)}, u32[]{:S(2)}) copy-start(f32[8,16,128]{2,1,0:T(8,128)} %mom_ref.1) | copy-start | bytes 196612
  27.1 43.3 %all-to-all-start.1 = ((f32[32,2,128]{2,1,0:T(2,128)}), f32[32,2,128]{2,1,0:T(2,128)S(1)}, u32[]{:S(2)}, u32[]{:S(2)}) async-start(f32[32,2,128]{2,1,0:T(2,128)} %summed_copies.1), calls=%async_computation.1 | async-start | bytes 65536 | tf_op jit(solution)/shard_map/all_to_all | solution.py:303
  40.6 17.5 %collective-permute-start.2 = (f32[34,4,128]{2,1,0:T(4,128)S(1)}, f32[34,4,128]{2,1,0:T(4,128)S(1)}, u32[]{:S(2)}, u32[]{:S(2)}) collective-permute-start(f32[34,4,128]{2,1,0:T(4,128)S(1)} %get-tuple-element.20), channel_id=1, source_target_pairs={{0,8},{8,0},{1,9},{9,1},{2,10},{10,2},{3,11},{11,3},{4,12},{12,4},... | collective-permute-start | bytes 208904 | tf_op jit(solution)/shard_map/ppermute | solution.py:292
  53.0 17.4 %collective-permute-start = (f32[3,4,16,128]{3,2,1,0:T(8,128)S(1)}, f32[3,4,16,128]{3,2,1,0:T(8,128)S(1)}, u32[]{:S(2)}, u32[]{:S(2)}) collective-permute-start(f32[3,4,16,128]{3,2,1,0:T(8,128)S(1)} %get-tuple-element.18), channel_id=1, source_target_pairs={{0,64},{64,128},{128,192},{192,256},{256,320},{320,384},{384,448},... | collective-permute-start | bytes 294920 | tf_op jit(solution)/shard_map/ppermute | solution.py:286
  53.0 17.4 %collective-permute-start.1 = (f32[3,4,16,128]{3,2,1,0:T(8,128)S(1)}, f32[3,4,16,128]{3,2,1,0:T(8,128)S(1)}, u32[]{:S(2)}, u32[]{:S(2)}) collective-permute-start(f32[3,4,16,128]{3,2,1,0:T(8,128)S(1)} %get-tuple-element.19), channel_id=1, source_target_pairs={{0,960},{64,0},{128,64},{192,128},{256,192},{320,256},{384,320},{4... | collective-permute-start | bytes 294920 | tf_op jit(solution)/shard_map/ppermute | solution.py:286
  58.1 12.3 %collective-permute-start.3 = (f32[16,4,128]{2,1,0:T(4,128)S(1)}, f32[16,4,128]{2,1,0:T(4,128)S(1)}, u32[]{:S(2)}, u32[]{:S(2)}) collective-permute-start(f32[16,4,128]{2,1,0:T(4,128)S(1)} %get-tuple-element.22), channel_id=1, source_target_pairs={{0,16},{16,32},{32,48},{48,0},{8,56},{24,8},{40,24},{56,40},{1,17}... | collective-permute-start | bytes 98312 | tf_op jit(solution)/shard_map/ppermute | solution.py:299
  60.7 8.2 %collective-permute-start.4 = (f32[8,128]{1,0:T(8,128)S(1)}, f32[8,128]{1,0:T(8,128)S(1)}, u32[]{:S(2)}, u32[]{:S(2)}) collective-permute-start(f32[8,128]{1,0:T(8,128)S(1)} %get-tuple-element.23), channel_id=1, source_target_pairs={{0,1},{2,3},{4,5},{6,7},{1,0},{3,2},{5,4},{7,6},{8,9},{10,11},{12,... | collective-permute-start | bytes 12296 | tf_op jit(solution)/shard_map/ppermute | solution.py:292
  62.6 7.8 %collective-permute-start.5 = (f32[8,128]{1,0:T(8,128)S(1)}, f32[8,128]{1,0:T(8,128)S(1)}, u32[]{:S(2)}, u32[]{:S(2)}) collective-permute-start(f32[8,128]{1,0:T(8,128)S(1)} %get-tuple-element.24), channel_id=1, source_target_pairs={{1,2},{3,4},{5,6},{7,8},{9,10},{11,12},{13,14},{15,0},{2,1},{4,3},... | collective-permute-start | bytes 12296 | tf_op jit(solution)/shard_map/ppermute | solution.py:292

commit v6 on v4

--- a/solution.py
+++ b/solution.py
@@ -12,9 +12,8 @@
 GX = ("gx_0", "gx_1")
 GY = ("gy_0", "gy_1")
 GZ = ("gz",)
-FIRST_GROUP = ("gx_1", "gy_1", "gz")
-RING = ("gy_1", "gz")
-SECOND_GROUP = ("gx_0", "gy_0")
+FIRST_GROUP = ("gy_1", "gz")
+SECOND_GROUP = ("gx_0", "gx_1", "gy_0")
 
 FIRST_COEFFS = (0.8, -0.2, 4.0 / 105.0, -1.0 / 280.0)
 SECOND_COEFFS = (1.6, -0.2, 8.0 / 315.0, -1.0 / 560.0)
@@ -33,6 +32,12 @@
     return lax.rem(lax.axis_index(axis), 2) == 1
 
 
+def depth_places():
+    place, count = lax.axis_index("gz"), lax.axis_size("gz")
+    base = lax.axis_index("gy_1") * count
+    return base + lax.rem(place + 1, count), base + lax.rem(place + count - 1, count)
+
+
 def angles(wave, start, step, count, total):
     index = lax.broadcasted_iota(jnp.int32, (count, LANES), 0)
     position = (start + step * index).astype(jnp.float32)
@@ -44,7 +49,7 @@
 def partial_kernel(
     full, copies, dens_hbm, mom_hbm, fuel_hbm, modes_hbm,
     part_ref, cos_ref, sin_ref, depth_ref,
-    xlo_ref, xhi_ref, sides_ref, za_ref, zb_ref,
+    xlo_ref, xhi_ref, sides_ref,
     dens_ref, mom_ref, fuel_ref, modes_ref, sems,
 ):
     size_x, size_y, size_z = mom_ref.shape
@@ -99,9 +104,9 @@
     part_cos = jnp.sum(cos_xy * real - sin_xy * imag, axis=0, keepdims=True)
     part_sin = jnp.sum(sin_xy * real + cos_xy * imag, axis=0, keepdims=True)
     both = jnp.concatenate([part_cos, part_sin], axis=0)
-    part_ref[...] = jnp.broadcast_to(both[None], (copies, 2, LANES))
+    part_ref[:, 0] = jnp.broadcast_to(both[None], (copies, 2, LANES))
     loads[3].wait()
-    odd_y, odd_z = odd("gy_1"), odd("gz")
+    odd_y = odd("gy_1")
     for n, ref in enumerate((dens_ref, mom_ref, fuel_ref)):
         xlo_ref[n] = ref[0:half]
         xhi_ref[n] = ref[size_x - half : size_x]
@@ -112,23 +117,24 @@
     turned = [ref[...].reshape(rows, size_z).T for ref in (mom_ref, fuel_ref)]
     low = jnp.concatenate([t[0:half] for t in turned], axis=0)
     high = jnp.concatenate([t[size_z - half : size_z] for t in turned], axis=0)
-    za_ref[...] = jnp.where(odd_z, low, high)
-    zb_ref[...] = jnp.where(odd_z, high, low)
+    following, _ = depth_places()
+    for n in range(4):
+        pair = slice(2 * n, 2 * n + 2)
+        part_ref[:, 1 + n] = jnp.broadcast_to(low[pair][None], (copies, 2, LANES))
+        part_ref[pl.ds(following, 1), 1 + n] = high[pair][None]
 
 
 def partial_sums(density, momentum, hydrogen, modes, full, copies):
     size_x, size_y, size_z = density.shape
     f32 = jnp.float32
     shapes = (
-        (copies, 2, LANES),
+        (copies, 5, 2, LANES),
         (size_x, size_y, LANES),
         (size_x, size_y, LANES),
         (size_z, 2 * LANES),
         (3, 4, size_y, size_z),
         (3, 4, size_y, size_z),
         (4 * size_x, 4, size_z),
-        (8, size_x * size_y),
-        (8, size_x * size_y),
     )
     density, momentum, hydrogen, modes = (
         pltpu.with_memory_space_constraint(f, pltpu.HBM) for f in (density, momentum, hydrogen, modes)
@@ -145,37 +151,26 @@
     )(density, momentum, hydrogen, modes)
 
 
-def spread_kernel(parts_ref, out_ref):
-    out_ref[...] = jnp.broadcast_to(jnp.sum(parts_ref[...], axis=0, keepdims=True), out_ref.shape)
+def spread_kernel(parts_ref, out_ref, before_ref, after_ref):
+    total = jnp.sum(parts_ref[:, 0], axis=0, keepdims=True)
+    out_ref[...] = jnp.broadcast_to(total, out_ref.shape)
+    following, preceding = depth_places()
+    for n in range(4):
+        pair = slice(2 * n, 2 * n + 2)
+        before_ref[pair] = parts_ref[preceding, 1 + n]
+        after_ref[pair] = parts_ref[following, 1 + n]
 
 
 def summed_copies(parts, copies):
+    edge = jax.ShapeDtypeStruct((8, LANES), jnp.float32)
     return pl.pallas_call(
         spread_kernel,
-        out_shape=jax.ShapeDtypeStruct((copies,) + parts.shape[1:], jnp.float32),
+        out_shape=[jax.ShapeDtypeStruct((copies, 2, LANES), jnp.float32), edge, edge],
         in_specs=[VMEM],
-        out_specs=VMEM,
+        out_specs=[VMEM] * 3,
         compiler_params=pltpu.CompilerParams(vmem_limit_bytes=4 << 20),
         name="summed_copies",
     )(parts)
-
-
-def pack_kernel(sides_ref, depth_ref, out_ref):
-    count = sides_ref.shape[0]
-    out_ref[0:count] = sides_ref[...]
-    out_ref[count] = depth_ref[0:4]
-    out_ref[count + 1] = depth_ref[4:8]
-
-
-def packed(sides, depth):
-    return pl.pallas_call(
-        pack_kernel,
-        out_shape=jax.ShapeDtypeStruct((sides.shape[0] + 2,) + sides.shape[1:], jnp.float32),
-        in_specs=[VMEM] * 2,
-        out_specs=VMEM,
-        compiler_params=pltpu.CompilerParams(vmem_limit_bytes=4 << 20),
-        name="packed",
-    )(sides, depth)
 
 
 def first_diff(planes, at):
@@ -195,7 +190,7 @@
 
 def final_kernel(
     ncell, dens_ref, mom_ref, fuel_ref, summed_ref, cos_ref, sin_ref, depth_ref,
-    xbefore_ref, xafter_ref, traded_ref, relayed_ref, za_ref, zb_ref,
+    xbefore_ref, xafter_ref, traded_ref, relayed_ref, zbefore_ref, zafter_ref,
     dens_out, mom_out, fuel_out, force_ref,
 ):
     size_x, size_y, size_z = mom_ref.shape
@@ -214,14 +209,8 @@
         preferred_element_type=jnp.float32,
     ).reshape(size_x, size_y, size_z)
     gap = jnp.zeros((56, rows), jnp.float32)
-    odd_y, odd_z = odd("gy_1"), odd("gz")
-    place = lax.axis_index("gz")
-    at_end = jnp.logical_or(place == 0, place == lax.axis_size("gz") - 1)
-    za, zb = za_ref[...], zb_ref[...]
-    swapped = jnp.concatenate([traded_ref[4 * size_x], traded_ref[4 * size_x + 1]], axis=0)
-    zb = jnp.where(at_end, swapped, zb)
-    before = jnp.where(odd_z, za, zb)
-    after = jnp.where(odd_z, zb, za)
+    odd_y = odd("gy_1")
+    before, after = zbefore_ref[...], zafter_ref[...]
     turned = jnp.concatenate(
         [after[0:4], gap, before[4:8], after[4:8], gap, before[0:4]], axis=0
     ).T
@@ -306,21 +295,18 @@
         size_z * lax.axis_size(GZ),
     )
     first, second = lax.axis_size(FIRST_GROUP), lax.axis_size(SECOND_GROUP)
-    part, cos, sin, depth, xlo, xhi, sides, za, zb = partial_sums(
+    part, cos, sin, depth, xlo, xhi, sides = partial_sums(
         density, momentum, hydrogen, forced_modes.T, full, first
     )
-    zb = swap(zb, RING, 1)
     part = exchange(part, FIRST_GROUP)
-    sides = packed(sides, zb)
     traded = swap(sides, ("gy_1",), 0)
-    part = summed_copies(part, second)
+    part, zbefore, zafter = summed_copies(part, second)
     part = exchange(part, SECOND_GROUP)
     xbefore, xafter = shift(xhi, GX, 1), shift(xlo, GX, -1)
-    za = swap(za, GZ, 0)
     relayed = relay(traded[2 * size_x : 4 * size_x])
     rates = final_rates(
         density, momentum, hydrogen, part, cos, sin, depth,
-        (xbefore, xafter, traded, relayed, za, zb), float(full[0] * full[1] * full[2]),
+        (xbefore, xafter, traded, relayed, zbefore, zafter), float(full[0] * full[1] * full[2]),
     )
     return tuple(rates)
 

time: 65.5 us -> 69.7 us (1.064)
  the two profiles are of different devices: /device:TPU:2 before, /device:TPU:8 now
where the time goes in v6:
time: 69.7 us; the launch traced here: 69.3 us
  blocking collectives  31.8 us (46%)
  starting transfers between devices  19.8 us (28%)
  waiting for transfers between devices  13.7 us (20%)
  Pallas kernels  3.36 us (5%)
  between operations  0.71 us (1%)
    all_to_all x1, blocking collectives, exchange(): return lax.all_to_all(x, axes, 0, 0, tiled=True)  31.8 us
    all_to_all x1, starting transfers between devices, exchange(): return lax.all_to_all(x, axes, 0, 0, tiled=True)  10.7 us
    ppermute x1, waiting for transfers between devices, swap(): return lax.ppermute(x, axes, pairs + [(j, i) for i, j in pairs])  10 us
    ppermute x1, starting transfers between devices, swap(): return lax.ppermute(x, axes, pairs + [(j, i) for i, j in pairs])  3.95 us
    ppermute x1, waiting for transfers between devices, relay(): return lax.ppermute(x, GY, ups + downs)  3.64 us
    ppermute x1, starting transfers between devices, relay(): return lax.ppermute(x, GY, ups + downs)  3.36 us
    ppermute x2, starting transfers between devices, shift(): return lax.ppermute(x, axes, [(i, (i + by) % size) for i in range(size)])  1.75 us
  transfers between devices with their start and end apart: 5, of which 2 were waited for; matrix products, arithmetic and copies ran while one was open for 0% of the time, Pallas kernels for 0%

profile of v6, /device:TPU:8, one launch (start us, length us, event | category | flops | bytes accessed | tf_op | source)
XLA Modules:
  0.0 69.3 jit_solution(2551627366963319305)
XLA Ops:
  0.6 1.3 %partial_sums.1 = (f32[16,5,2,128]{3,2,1,0:T(2,128)S(1)}, f32[8,16,128]{2,1,0:T(8,128)S(1)}, f32[8,16,128]{2,1,0:T(8,128)S(1)}, f32[128,256]{1,0:T(8,128)S(1)}, ...) custom-call(f32[8,16,128]{2,1,0:T(8,128)} %dens_ref.1, ...), custom_call_target="tpu_custom_call" | custom-call | tf_op jit(solution)/shard_map/partial_sums/pallas_call | solution.py:142
  2.0 31.8 %all_to_all.10.parts_ref = f32[16,5,2,128]{3,2,1,0:T(2,128)S(1)} all-to-all(f32[16,5,2,128]{3,2,1,0:T(2,128)S(1)} %get-tuple-element.13), channel_id=1, replica_groups=mesh['gx_0'=8,'gx_1'=2,'gy_0'=4,'gy_1'=2,'gz'=8] {'gy_1','gz'}, dimensions={0} | all-to-all | bytes 163840 | tf_op jit(solution)/shard_map/all_to_all | solution.py:287
  33.8 0.7 summed_copies.1
  34.4 0.0 copy-start.1
  34.4 0.0 copy-start.2
  34.4 10.7 %all-to-all-start.1 = ((f32[64,2,128]{2,1,0:T(2,128)}), f32[64,2,128]{2,1,0:T(2,128)S(1)}, u32[]{:S(2)}, u32[]{:S(2)}) async-start(f32[64,2,128]{2,1,0:T(2,128)} %get-tuple-element.14), calls=%async_computation.1 | async-start | bytes 131072 | tf_op jit(solution)/shard_map/all_to_all | solution.py:287
  45.1 0.0 copy-start
  45.1 3.9 %collective-permute-start.2 = (f32[32,4,128]{2,1,0:T(4,128)S(1)}, f32[32,4,128]{2,1,0:T(4,128)S(1)}, u32[]{:S(2)}, u32[]{:S(2)}) collective-permute-start(f32[32,4,128]{2,1,0:T(4,128)S(1)} %get-tuple-element.20), channel_id=1, source_target_pairs={{0,8},{8,0},{1,9},{9,1},{2,10},{10,2},{3,11},{11,3},{4,12},{12,4},... | collective-permute-start | bytes 196616 | tf_op jit(solution)/shard_map/ppermute | solution.py:276
  49.1 0.0 collective-permute-start
  49.1 1.7 %collective-permute-start.1 = (f32[3,4,16,128]{3,2,1,0:T(8,128)S(1)}, f32[3,4,16,128]{3,2,1,0:T(8,128)S(1)}, u32[]{:S(2)}, u32[]{:S(2)}) collective-permute-start(f32[3,4,16,128]{3,2,1,0:T(8,128)S(1)} %get-tuple-element.19), channel_id=1, source_target_pairs={{0,960},{64,0},{128,64},{192,128},{256,192},{320,256},{384,320},{4... | collective-permute-start | bytes 294920 | tf_op jit(solution)/shard_map/ppermute | solution.py:270
  50.9 10.0 %collective-permute-done.2.traded_ref = f32[32,4,128]{2,1,0:T(4,128)S(1)} collective-permute-done((f32[32,4,128]{2,1,0:T(4,128)S(1)}, f32[32,4,128]{2,1,0:T(4,128)S(1)}, u32[]{:S(2)}, u32[]{:S(2)}) %collective-permute-start.2) | collective-permute-done | bytes 65568 | tf_op jit(solution)/shard_map/ppermute | solution.py:276
  60.9 3.4 %collective-permute-start.3 = (f32[16,4,128]{2,1,0:T(4,128)S(1)}, f32[16,4,128]{2,1,0:T(4,128)S(1)}, u32[]{:S(2)}, u32[]{:S(2)}) collective-permute-start(f32[16,4,128]{2,1,0:T(4,128)S(1)} %slice.4), channel_id=1, source_target_pairs={{0,16},{16,32},{32,48},{48,0},{8,56},{24,8},{40,24},{56,40},{1,17}... | collective-permute-start | bytes 98312 | tf_op jit(solution)/shard_map/ppermute | solution.py:283
  64.3 3.6 %collective-permute-done.3.relayed_ref = f32[16,4,128]{2,1,0:T(4,128)S(1)} collective-permute-done((f32[16,4,128]{2,1,0:T(4,128)S(1)}, f32[16,4,128]{2,1,0:T(4,128)S(1)}, u32[]{:S(2)}, u32[]{:S(2)}) %collective-permute-start.3) | collective-permute-done | bytes 32800 | tf_op jit(solution)/shard_map/ppermute | solution.py:283
  67.9 0.0 collective-permute-done.xbefore_ref
  67.9 0.0 collective-permute-done.1.xafter_ref
  67.9 0.0 all-to-all-done.1.summed_ref
  67.9 0.0 copy-done.1
  67.9 0.0 copy-done.2
  67.9 0.0 copy-done
  68.0 1.4 %final_rates.1 = (f32[8,16,128]{2,1,0:T(8,128)}, f32[8,16,128]{2,1,0:T(8,128)}, f32[8,16,128]{2,1,0:T(8,128)}) custom-call(f32[8,16,128]{2,1,0:T(8,128)S(1)} %copy-done, f32[8,16,128]{2,1,0:T(8,128)S(1)} %copy-done.1, f32[8,16,128]{2,1,0:T(8,128)S(1)} %copy-done.2, f32[64,2,128]{2,1,0:T(2,128)S(1)} %all-to-all-done.1.summed_ref, ...), custom_call_target="tpu_custom_call" | custom-call | tf_op jit(solution)/shard_map/final_rates/pallas_call | solution.py:257
  (1 shorter events, 0.0 us)
Async XLA Ops:
  34.4 33.5 %copy-start.1 = (f32[8,16,128]{2,1,0:T(8,128)S(1)}, f32[8,16,128]{2,1,0:T(8,128)}, u32[]{:S(2)}) copy-start(f32[8,16,128]{2,1,0:T(8,128)} %mom_ref.1) | copy-start | bytes 196612
  34.4 33.5 %copy-start.2 = (f32[8,16,128]{2,1,0:T(8,128)S(1)}, f32[8,16,128]{2,1,0:T(8,128)}, u32[]{:S(2)}) copy-start(f32[8,16,128]{2,1,0:T(8,128)} %fuel_ref.1) | copy-start | bytes 196612
  34.4 33.5 %all-to-all-start.1 = ((f32[64,2,128]{2,1,0:T(2,128)}), f32[64,2,128]{2,1,0:T(2,128)S(1)}, u32[]{:S(2)}, u32[]{:S(2)}) async-start(f32[64,2,128]{2,1,0:T(2,128)} %get-tuple-element.14), calls=%async_computation.1 | async-start | bytes 131072 | tf_op jit(solution)/shard_map/all_to_all | solution.py:287
  45.1 22.8 %copy-start = (f32[8,16,128]{2,1,0:T(8,128)S(1)}, f32[8,16,128]{2,1,0:T(8,128)}, u32[]{:S(2)}) copy-start(f32[8,16,128]{2,1,0:T(8,128)} %dens_ref.1) | copy-start | bytes 196612
  45.1 15.8 %collective-permute-start.2 = (f32[32,4,128]{2,1,0:T(4,128)S(1)}, f32[32,4,128]{2,1,0:T(4,128)S(1)}, u32[]{:S(2)}, u32[]{:S(2)}) collective-permute-start(f32[32,4,128]{2,1,0:T(4,128)S(1)} %get-tuple-element.20), channel_id=1, source_target_pairs={{0,8},{8,0},{1,9},{9,1},{2,10},{10,2},{3,11},{11,3},{4,12},{12,4},... | collective-permute-start | bytes 196616 | tf_op jit(solution)/shard_map/ppermute | solution.py:276
  49.1 18.8 %collective-permute-start = (f32[3,4,16,128]{3,2,1,0:T(8,128)S(1)}, f32[3,4,16,128]{3,2,1,0:T(8,128)S(1)}, u32[]{:S(2)}, u32[]{:S(2)}) collective-permute-start(f32[3,4,16,128]{3,2,1,0:T(8,128)S(1)} %get-tuple-element.18), channel_id=1, source_target_pairs={{0,64},{64,128},{128,192},{192,256},{256,320},{320,384},{384,448},... | collective-permute-start | bytes 294920 | tf_op jit(solution)/shard_map/ppermute | solution.py:270
  49.1 18.8 %collective-permute-start.1 = (f32[3,4,16,128]{3,2,1,0:T(8,128)S(1)}, f32[3,4,16,128]{3,2,1,0:T(8,128)S(1)}, u32[]{:S(2)}, u32[]{:S(2)}) collective-permute-start(f32[3,4,16,128]{3,2,1,0:T(8,128)S(1)} %get-tuple-element.19), channel_id=1, source_target_pairs={{0,960},{64,0},{128,64},{192,128},{256,192},{320,256},{384,320},{4... | collective-permute-start | bytes 294920 | tf_op jit(solution)/shard_map/ppermute | solution.py:270
  60.9 7.0 %collective-permute-start.3 = (f32[16,4,128]{2,1,0:T(4,128)S(1)}, f32[16,4,128]{2,1,0:T(4,128)S(1)}, u32[]{:S(2)}, u32[]{:S(2)}) collective-permute-start(f32[16,4,128]{2,1,0:T(4,128)S(1)} %slice.4), channel_id=1, source_target_pairs={{0,16},{16,32},{32,48},{48,0},{8,56},{24,8},{40,24},{56,40},{1,17}... | collective-permute-start | bytes 98312 | tf_op jit(solution)/shard_map/ppermute | solution.py:283

commit v7 on v6

--- a/solution.py
+++ b/solution.py
@@ -13,6 +13,7 @@
 GY = ("gy_0", "gy_1")
 GZ = ("gz",)
 FIRST_GROUP = ("gy_1", "gz")
+FIRST_MEMBER = 8
 SECOND_GROUP = ("gx_0", "gx_1", "gy_0")
 
 FIRST_COEFFS = (0.8, -0.2, 4.0 / 105.0, -1.0 / 280.0)
@@ -34,8 +35,9 @@
 
 def depth_places():
     place, count = lax.axis_index("gz"), lax.axis_size("gz")
-    base = lax.axis_index("gy_1") * count
-    return base + lax.rem(place + 1, count), base + lax.rem(place + count - 1, count)
+    whole = count * lax.axis_size("gy_1")
+    base = lax.axis_index("gy_1") * count + whole - FIRST_MEMBER
+    return tuple(lax.rem(base + lax.rem(place + by, count), whole) for by in (1, count - 1))
 
 
 def angles(wave, start, step, count, total):
@@ -283,8 +285,8 @@
     return lax.ppermute(x, GY, ups + downs)
 
 
-def exchange(x, axes):
-    return lax.all_to_all(x, axes, 0, 0, tiled=True)
+def exchange(x, axes, groups=None):
+    return lax.all_to_all(x, axes, 0, 0, axis_index_groups=groups, tiled=True)
 
 
 def per_device(density, momentum, hydrogen, forced_modes):
@@ -298,7 +300,8 @@
     part, cos, sin, depth, xlo, xhi, sides = partial_sums(
         density, momentum, hydrogen, forced_modes.T, full, first
     )
-    part = exchange(part, FIRST_GROUP)
+    order = [(FIRST_MEMBER + i) % first for i in range(first)]
+    part = exchange(part, FIRST_GROUP, [order])
     traded = swap(sides, ("gy_1",), 0)
     part, zbefore, zafter = summed_copies(part, second)
     part = exchange(part, SECOND_GROUP)

time: 69.7 us -> 67.2 us (0.964)
  waiting for transfers between devices: 13.7 us -> 6.14 us
  starting transfers between devices: 19.8 us -> 26.8 us
  blocking collectives: 31.8 us -> 29.9 us
    ppermute x1, waiting for transfers between devices: 10 us -> 2.5 us  [swap(): return lax.ppermute(x, axes, pairs + [(j, i) for i, j in pairs])]
    ppermute x1, starting transfers between devices: 3.95 us -> 10.9 us  [swap(): return lax.ppermute(x, axes, pairs + [(j, i) for i, j in pairs])]
    all_to_all x1, blocking collectives: 31.8 us -> 29.9 us  [exchange(): return lax.all_to_all(x, axes, 0, 0, axis_index_groups=groups, tiled=True)]
where the time goes in v7:
time: 67.2 us; the launch traced here: 66.9 us
  blocking collectives  29.9 us (44%)
  starting transfers between devices  26.8 us (40%)
  waiting for transfers between devices  6.14 us (9%)
  Pallas kernels  3.36 us (5%)
  between operations  0.71 us (1%)
    all_to_all x1, blocking collectives, exchange(): return lax.all_to_all(x, axes, 0, 0, axis_index_groups=groups, tiled=True)  29.9 us
    ppermute x1, starting transfers between devices, swap(): return lax.ppermute(x, axes, pairs + [(j, i) for i, j in pairs])  10.9 us
    all_to_all x1, starting transfers between devices, exchange(): return lax.all_to_all(x, axes, 0, 0, axis_index_groups=groups, tiled=True)  10.7 us
    ppermute x1, waiting for transfers between devices, relay(): return lax.ppermute(x, GY, ups + downs)  3.64 us
    ppermute x1, starting transfers between devices, relay(): return lax.ppermute(x, GY, ups + downs)  3.36 us
    ppermute x1, waiting for transfers between devices, swap(): return lax.ppermute(x, axes, pairs + [(j, i) for i, j in pairs])  2.5 us
    ppermute x2, starting transfers between devices, shift(): return lax.ppermute(x, axes, [(i, (i + by) % size) for i in range(size)])  1.75 us
    pallas_call x1, Pallas kernels, final_rates(): pl.pallas_call(functools.partial(final_kernel, ncell), out_shape=[jax.Sha...  1.37 us
  transfers between devices with their start and end apart: 5, of which 2 were waited for; matrix products, arithmetic and copies ran while one was open for 0% of the time, Pallas kernels for 0%

profile of v7, /device:TPU:8, one launch (start us, length us, event | category | flops | bytes accessed | tf_op | source)
XLA Modules:
  0.0 66.9 jit_solution(13371803591457270634)
XLA Ops:
  0.6 1.3 %partial_sums.1 = (f32[16,5,2,128]{3,2,1,0:T(2,128)S(1)}, f32[8,16,128]{2,1,0:T(8,128)S(1)}, f32[8,16,128]{2,1,0:T(8,128)S(1)}, f32[128,256]{1,0:T(8,128)S(1)}, ...) custom-call(f32[8,16,128]{2,1,0:T(8,128)} %dens_ref.1, ...), custom_call_target="tpu_custom_call" | custom-call | tf_op jit(solution)/shard_map/partial_sums/pallas_call | solution.py:144
  2.0 29.9 %all_to_all.10.parts_ref = f32[16,5,2,128]{3,2,1,0:T(2,128)S(1)} all-to-all(f32[16,5,2,128]{3,2,1,0:T(2,128)S(1)} %get-tuple-element.13), channel_id=1, replica_groups={{8,9,10,11,12,13,14,15,0,1,2,3,4,5,6,7},{24,25,26,27,28,29,30,31,16,17,..., dimensions={0} | all-to-all | bytes 163840 | tf_op jit(solution)/shard_map/all_to_all | solution.py:289
  31.8 0.7 summed_copies.1
  32.5 0.0 copy-start.1
  32.5 0.0 copy-start.2
  32.5 10.7 %all-to-all-start.1 = ((f32[64,2,128]{2,1,0:T(2,128)}), f32[64,2,128]{2,1,0:T(2,128)S(1)}, u32[]{:S(2)}, u32[]{:S(2)}) async-start(f32[64,2,128]{2,1,0:T(2,128)} %get-tuple-element.14), calls=%async_computation.1 | async-start | bytes 131072 | tf_op jit(solution)/shard_map/all_to_all | solution.py:289
  43.2 0.0 copy-start
  43.2 10.9 %collective-permute-start.2 = (f32[32,4,128]{2,1,0:T(4,128)S(1)}, f32[32,4,128]{2,1,0:T(4,128)S(1)}, u32[]{:S(2)}, u32[]{:S(2)}) collective-permute-start(f32[32,4,128]{2,1,0:T(4,128)S(1)} %get-tuple-element.20), channel_id=1, source_target_pairs={{0,8},{8,0},{1,9},{9,1},{2,10},{10,2},{3,11},{11,3},{4,12},{12,4},... | collective-permute-start | bytes 196616 | tf_op jit(solution)/shard_map/ppermute | solution.py:278
  54.2 0.0 collective-permute-start
  54.2 1.7 %collective-permute-start.1 = (f32[3,4,16,128]{3,2,1,0:T(8,128)S(1)}, f32[3,4,16,128]{3,2,1,0:T(8,128)S(1)}, u32[]{:S(2)}, u32[]{:S(2)}) collective-permute-start(f32[3,4,16,128]{3,2,1,0:T(8,128)S(1)} %get-tuple-element.19), channel_id=1, source_target_pairs={{0,960},{64,0},{128,64},{192,128},{256,192},{320,256},{384,320},{4... | collective-permute-start | bytes 294920 | tf_op jit(solution)/shard_map/ppermute | solution.py:272
  55.9 2.5 %collective-permute-done.2.traded_ref = f32[32,4,128]{2,1,0:T(4,128)S(1)} collective-permute-done((f32[32,4,128]{2,1,0:T(4,128)S(1)}, f32[32,4,128]{2,1,0:T(4,128)S(1)}, u32[]{:S(2)}, u32[]{:S(2)}) %collective-permute-start.2) | collective-permute-done | bytes 65568 | tf_op jit(solution)/shard_map/ppermute | solution.py:278
  58.4 3.4 %collective-permute-start.3 = (f32[16,4,128]{2,1,0:T(4,128)S(1)}, f32[16,4,128]{2,1,0:T(4,128)S(1)}, u32[]{:S(2)}, u32[]{:S(2)}) collective-permute-start(f32[16,4,128]{2,1,0:T(4,128)S(1)} %slice.4), channel_id=1, source_target_pairs={{0,16},{16,32},{32,48},{48,0},{8,56},{24,8},{40,24},{56,40},{1,17}... | collective-permute-start | bytes 98312 | tf_op jit(solution)/shard_map/ppermute | solution.py:285
  61.8 3.6 %collective-permute-done.3.relayed_ref = f32[16,4,128]{2,1,0:T(4,128)S(1)} collective-permute-done((f32[16,4,128]{2,1,0:T(4,128)S(1)}, f32[16,4,128]{2,1,0:T(4,128)S(1)}, u32[]{:S(2)}, u32[]{:S(2)}) %collective-permute-start.3) | collective-permute-done | bytes 32800 | tf_op jit(solution)/shard_map/ppermute | solution.py:285
  65.4 0.0 collective-permute-done.xbefore_ref
  65.4 0.0 collective-permute-done.1.xafter_ref
  65.4 0.0 all-to-all-done.1.summed_ref
  65.5 0.0 copy-done.1
  65.5 0.0 copy-done.2
  65.5 0.0 copy-done
  65.5 1.4 %final_rates.1 = (f32[8,16,128]{2,1,0:T(8,128)}, f32[8,16,128]{2,1,0:T(8,128)}, f32[8,16,128]{2,1,0:T(8,128)}) custom-call(f32[8,16,128]{2,1,0:T(8,128)S(1)} %copy-done, f32[8,16,128]{2,1,0:T(8,128)S(1)} %copy-done.1, f32[8,16,128]{2,1,0:T(8,128)S(1)} %copy-done.2, f32[64,2,128]{2,1,0:T(2,128)S(1)} %all-to-all-done.1.summed_ref, ...), custom_call_target="tpu_custom_call" | custom-call | tf_op jit(solution)/shard_map/final_rates/pallas_call | solution.py:259
  (1 shorter events, 0.0 us)
Async XLA Ops:
  32.5 33.0 %copy-start.1 = (f32[8,16,128]{2,1,0:T(8,128)S(1)}, f32[8,16,128]{2,1,0:T(8,128)}, u32[]{:S(2)}) copy-start(f32[8,16,128]{2,1,0:T(8,128)} %mom_ref.1) | copy-start | bytes 196612
  32.5 33.0 %copy-start.2 = (f32[8,16,128]{2,1,0:T(8,128)S(1)}, f32[8,16,128]{2,1,0:T(8,128)}, u32[]{:S(2)}) copy-start(f32[8,16,128]{2,1,0:T(8,128)} %fuel_ref.1) | copy-start | bytes 196612
  32.5 32.9 %all-to-all-start.1 = ((f32[64,2,128]{2,1,0:T(2,128)}), f32[64,2,128]{2,1,0:T(2,128)S(1)}, u32[]{:S(2)}, u32[]{:S(2)}) async-start(f32[64,2,128]{2,1,0:T(2,128)} %get-tuple-element.14), calls=%async_computation.1 | async-start | bytes 131072 | tf_op jit(solution)/shard_map/all_to_all | solution.py:289
  43.2 22.3 %copy-start = (f32[8,16,128]{2,1,0:T(8,128)S(1)}, f32[8,16,128]{2,1,0:T(8,128)}, u32[]{:S(2)}) copy-start(f32[8,16,128]{2,1,0:T(8,128)} %dens_ref.1) | copy-start | bytes 196612
  43.2 15.2 %collective-permute-start.2 = (f32[32,4,128]{2,1,0:T(4,128)S(1)}, f32[32,4,128]{2,1,0:T(4,128)S(1)}, u32[]{:S(2)}, u32[]{:S(2)}) collective-permute-start(f32[32,4,128]{2,1,0:T(4,128)S(1)} %get-tuple-element.20), channel_id=1, source_target_pairs={{0,8},{8,0},{1,9},{9,1},{2,10},{10,2},{3,11},{11,3},{4,12},{12,4},... | collective-permute-start | bytes 196616 | tf_op jit(solution)/shard_map/ppermute | solution.py:278
  54.2 11.3 %collective-permute-start = (f32[3,4,16,128]{3,2,1,0:T(8,128)S(1)}, f32[3,4,16,128]{3,2,1,0:T(8,128)S(1)}, u32[]{:S(2)}, u32[]{:S(2)}) collective-permute-start(f32[3,4,16,128]{3,2,1,0:T(8,128)S(1)} %get-tuple-element.18), channel_id=1, source_target_pairs={{0,64},{64,128},{128,192},{192,256},{256,320},{320,384},{384,448},... | collective-permute-start | bytes 294920 | tf_op jit(solution)/shard_map/ppermute | solution.py:272
  54.2 11.2 %collective-permute-start.1 = (f32[3,4,16,128]{3,2,1,0:T(8,128)S(1)}, f32[3,4,16,128]{3,2,1,0:T(8,128)S(1)}, u32[]{:S(2)}, u32[]{:S(2)}) collective-permute-start(f32[3,4,16,128]{3,2,1,0:T(8,128)S(1)} %get-tuple-element.19), channel_id=1, source_target_pairs={{0,960},{64,0},{128,64},{192,128},{256,192},{320,256},{384,320},{4... | collective-permute-start | bytes 294920 | tf_op jit(solution)/shard_map/ppermute | solution.py:272
  58.4 7.0 %collective-permute-start.3 = (f32[16,4,128]{2,1,0:T(4,128)S(1)}, f32[16,4,128]{2,1,0:T(4,128)S(1)}, u32[]{:S(2)}, u32[]{:S(2)}) collective-permute-start(f32[16,4,128]{2,1,0:T(4,128)S(1)} %slice.4), channel_id=1, source_target_pairs={{0,16},{16,32},{32,48},{48,0},{8,56},{24,8},{40,24},{56,40},{1,17}... | collective-permute-start | bytes 98312 | tf_op jit(solution)/shard_map/ppermute | solution.py:285

commit v8 on v7

--- a/solution.py
+++ b/solution.py
@@ -14,6 +14,7 @@
 GZ = ("gz",)
 FIRST_GROUP = ("gy_1", "gz")
 FIRST_MEMBER = 8
+PLANE_MEMBER = 32
 SECOND_GROUP = ("gx_0", "gx_1", "gy_0")
 
 FIRST_COEFFS = (0.8, -0.2, 4.0 / 105.0, -1.0 / 280.0)
@@ -285,8 +286,10 @@
     return lax.ppermute(x, GY, ups + downs)
 
 
-def exchange(x, axes, groups=None):
-    return lax.all_to_all(x, axes, 0, 0, axis_index_groups=groups, tiled=True)
+def exchange(x, axes, member):
+    size = lax.axis_size(axes)
+    order = [(member + i) % size for i in range(size)]
+    return lax.all_to_all(x, axes, 0, 0, axis_index_groups=[order], tiled=True)
 
 
 def per_device(density, momentum, hydrogen, forced_modes):
@@ -300,12 +303,11 @@
     part, cos, sin, depth, xlo, xhi, sides = partial_sums(
         density, momentum, hydrogen, forced_modes.T, full, first
     )
-    order = [(FIRST_MEMBER + i) % first for i in range(first)]
-    part = exchange(part, FIRST_GROUP, [order])
+    part = exchange(part, FIRST_GROUP, FIRST_MEMBER)
     traded = swap(sides, ("gy_1",), 0)
+    xbefore, xafter = shift(xhi, GX, 1), shift(xlo, GX, -1)
     part, zbefore, zafter = summed_copies(part, second)
-    part = exchange(part, SECOND_GROUP)
-    xbefore, xafter = shift(xhi, GX, 1), shift(xlo, GX, -1)
+    part = exchange(part, SECOND_GROUP, PLANE_MEMBER)
     relayed = relay(traded[2 * size_x : 4 * size_x])
     rates = final_rates(
         density, momentum, hydrogen, part, cos, sin, depth,

time: 67.2 us -> 67.8 us (level)
  the two profiles are of different devices: /device:TPU:8 before, /device:TPU:256 now
where the time goes in v8:
time: 67.8 us; the launch traced here: 67.4 us
  blocking collectives  26 us (38%)
  starting transfers between devices  25 us (37%)
  waiting for transfers between devices  12.4 us (18%)
  Pallas kernels  3.35 us (5%)
  between operations  0.71 us (1%)
    all_to_all x1, blocking collectives, exchange(): return lax.all_to_all(x, axes, 0, 0, axis_index_groups=[order], tiled=True)  26 us
    all_to_all x1, starting transfers between devices, exchange(): return lax.all_to_all(x, axes, 0, 0, axis_index_groups=[order], tiled=True)  11.2 us
    ppermute x1, waiting for transfers between devices, swap(): return lax.ppermute(x, axes, pairs + [(j, i) for i, j in pairs])  8.74 us
    ppermute x1, starting transfers between devices, swap(): return lax.ppermute(x, axes, pairs + [(j, i) for i, j in pairs])  7.42 us
    ppermute x1, waiting for transfers between devices, relay(): return lax.ppermute(x, GY, ups + downs)  3.63 us
    ppermute x1, starting transfers between devices, relay(): return lax.ppermute(x, GY, ups + downs)  3.37 us
    ppermute x2, starting transfers between devices, shift(): return lax.ppermute(x, axes, [(i, (i + by) % size) for i in range(size)])  2.96 us
    pallas_call x1, Pallas kernels, final_rates(): pl.pallas_call(functools.partial(final_kernel, ncell), out_shape=[jax.Sha...  1.37 us
  transfers between devices with their start and end apart: 5, of which 2 were waited for; matrix products, arithmetic and copies ran while one was open for 0% of the time, Pallas kernels for 0%

profile of v8, /device:TPU:256, one launch (start us, length us, event | category | flops | bytes accessed | tf_op | source)
XLA Modules:
  0.0 67.4 jit_solution(3128447149101328629)
XLA Ops:
  0.6 1.3 %partial_sums.1 = (f32[16,5,2,128]{3,2,1,0:T(2,128)S(1)}, f32[8,16,128]{2,1,0:T(8,128)S(1)}, f32[8,16,128]{2,1,0:T(8,128)S(1)}, f32[128,256]{1,0:T(8,128)S(1)}, ...) custom-call(f32[8,16,128]{2,1,0:T(8,128)} %dens_ref.1, ...), custom_call_target="tpu_custom_call" | custom-call | tf_op jit(solution)/shard_map/partial_sums/pallas_call | solution.py:145
  2.0 26.0 %all_to_all.10.parts_ref = f32[16,5,2,128]{3,2,1,0:T(2,128)S(1)} all-to-all(f32[16,5,2,128]{3,2,1,0:T(2,128)S(1)} %get-tuple-element.13), channel_id=1, replica_groups={{8,9,10,11,12,13,14,15,0,1,2,3,4,5,6,7},{24,25,26,27,28,29,30,31,16,17,..., dimensions={0} | all-to-all | bytes 163840 | tf_op jit(solution)/shard_map/all_to_all | solution.py:292
  27.9 0.7 summed_copies.1
  28.6 0.0 copy-start.1
  28.6 0.0 copy-start.2
  28.6 11.2 %all-to-all-start.1 = ((f32[64,2,128]{2,1,0:T(2,128)}), f32[64,2,128]{2,1,0:T(2,128)S(1)}, u32[]{:S(2)}, u32[]{:S(2)}) async-start(f32[64,2,128]{2,1,0:T(2,128)} %get-tuple-element.14), calls=%async_computation.1 | async-start | bytes 131072 | tf_op jit(solution)/shard_map/all_to_all | solution.py:292
  39.8 0.0 copy-start
  39.8 7.4 %collective-permute-start.2 = (f32[32,4,128]{2,1,0:T(4,128)S(1)}, f32[32,4,128]{2,1,0:T(4,128)S(1)}, u32[]{:S(2)}, u32[]{:S(2)}) collective-permute-start(f32[32,4,128]{2,1,0:T(4,128)S(1)} %get-tuple-element.20), channel_id=1, source_target_pairs={{0,8},{8,0},{1,9},{9,1},{2,10},{10,2},{3,11},{11,3},{4,12},{12,4},... | collective-permute-start | bytes 196616 | tf_op jit(solution)/shard_map/ppermute | solution.py:279
  47.3 0.0 collective-permute-start
  47.3 2.9 %collective-permute-start.1 = (f32[3,4,16,128]{3,2,1,0:T(8,128)S(1)}, f32[3,4,16,128]{3,2,1,0:T(8,128)S(1)}, u32[]{:S(2)}, u32[]{:S(2)}) collective-permute-start(f32[3,4,16,128]{3,2,1,0:T(8,128)S(1)} %get-tuple-element.19), channel_id=1, source_target_pairs={{0,960},{64,0},{128,64},{192,128},{256,192},{320,256},{384,320},{4... | collective-permute-start | bytes 294920 | tf_op jit(solution)/shard_map/ppermute | solution.py:273
  50.2 8.7 %collective-permute-done.2.traded_ref = f32[32,4,128]{2,1,0:T(4,128)S(1)} collective-permute-done((f32[32,4,128]{2,1,0:T(4,128)S(1)}, f32[32,4,128]{2,1,0:T(4,128)S(1)}, u32[]{:S(2)}, u32[]{:S(2)}) %collective-permute-start.2) | collective-permute-done | bytes 65568 | tf_op jit(solution)/shard_map/ppermute | solution.py:279
  59.0 3.4 %collective-permute-start.3 = (f32[16,4,128]{2,1,0:T(4,128)S(1)}, f32[16,4,128]{2,1,0:T(4,128)S(1)}, u32[]{:S(2)}, u32[]{:S(2)}) collective-permute-start(f32[16,4,128]{2,1,0:T(4,128)S(1)} %slice.4), channel_id=1, source_target_pairs={{0,16},{16,32},{32,48},{48,0},{8,56},{24,8},{40,24},{56,40},{1,17}... | collective-permute-start | bytes 98312 | tf_op jit(solution)/shard_map/ppermute | solution.py:286
  62.4 3.6 %collective-permute-done.3.relayed_ref = f32[16,4,128]{2,1,0:T(4,128)S(1)} collective-permute-done((f32[16,4,128]{2,1,0:T(4,128)S(1)}, f32[16,4,128]{2,1,0:T(4,128)S(1)}, u32[]{:S(2)}, u32[]{:S(2)}) %collective-permute-start.3) | collective-permute-done | bytes 32800 | tf_op jit(solution)/shard_map/ppermute | solution.py:286
  66.0 0.0 collective-permute-done.xbefore_ref
  66.0 0.0 collective-permute-done.1.xafter_ref
  66.0 0.0 all-to-all-done.1.summed_ref
  66.0 0.0 copy-done.1
  66.0 0.0 copy-done.2
  66.0 0.0 copy-done
  66.0 1.4 %final_rates.1 = (f32[8,16,128]{2,1,0:T(8,128)}, f32[8,16,128]{2,1,0:T(8,128)}, f32[8,16,128]{2,1,0:T(8,128)}) custom-call(f32[8,16,128]{2,1,0:T(8,128)S(1)} %copy-done, f32[8,16,128]{2,1,0:T(8,128)S(1)} %copy-done.1, f32[8,16,128]{2,1,0:T(8,128)S(1)} %copy-done.2, f32[64,2,128]{2,1,0:T(2,128)S(1)} %all-to-all-done.1.summed_ref, ...), custom_call_target="tpu_custom_call" | custom-call | tf_op jit(solution)/shard_map/final_rates/pallas_call | solution.py:260
  (1 shorter events, 0.0 us)
Async XLA Ops:
  28.6 37.4 %copy-start.1 = (f32[8,16,128]{2,1,0:T(8,128)S(1)}, f32[8,16,128]{2,1,0:T(8,128)}, u32[]{:S(2)}) copy-start(f32[8,16,128]{2,1,0:T(8,128)} %mom_ref.1) | copy-start | bytes 196612
  28.6 37.4 %copy-start.2 = (f32[8,16,128]{2,1,0:T(8,128)S(1)}, f32[8,16,128]{2,1,0:T(8,128)}, u32[]{:S(2)}) copy-start(f32[8,16,128]{2,1,0:T(8,128)} %fuel_ref.1) | copy-start | bytes 196612
  28.6 37.4 %all-to-all-start.1 = ((f32[64,2,128]{2,1,0:T(2,128)}), f32[64,2,128]{2,1,0:T(2,128)S(1)}, u32[]{:S(2)}, u32[]{:S(2)}) async-start(f32[64,2,128]{2,1,0:T(2,128)} %get-tuple-element.14), calls=%async_computation.1 | async-start | bytes 131072 | tf_op jit(solution)/shard_map/all_to_all | solution.py:292
  39.8 26.2 %copy-start = (f32[8,16,128]{2,1,0:T(8,128)S(1)}, f32[8,16,128]{2,1,0:T(8,128)}, u32[]{:S(2)}) copy-start(f32[8,16,128]{2,1,0:T(8,128)} %dens_ref.1) | copy-start | bytes 196612
  39.8 19.1 %collective-permute-start.2 = (f32[32,4,128]{2,1,0:T(4,128)S(1)}, f32[32,4,128]{2,1,0:T(4,128)S(1)}, u32[]{:S(2)}, u32[]{:S(2)}) collective-permute-start(f32[32,4,128]{2,1,0:T(4,128)S(1)} %get-tuple-element.20), channel_id=1, source_target_pairs={{0,8},{8,0},{1,9},{9,1},{2,10},{10,2},{3,11},{11,3},{4,12},{12,4},... | collective-permute-start | bytes 196616 | tf_op jit(solution)/shard_map/ppermute | solution.py:279
  47.3 18.7 %collective-permute-start = (f32[3,4,16,128]{3,2,1,0:T(8,128)S(1)}, f32[3,4,16,128]{3,2,1,0:T(8,128)S(1)}, u32[]{:S(2)}, u32[]{:S(2)}) collective-permute-start(f32[3,4,16,128]{3,2,1,0:T(8,128)S(1)} %get-tuple-element.18), channel_id=1, source_target_pairs={{0,64},{64,128},{128,192},{192,256},{256,320},{320,384},{384,448},... | collective-permute-start | bytes 294920 | tf_op jit(solution)/shard_map/ppermute | solution.py:273
  47.3 18.7 %collective-permute-start.1 = (f32[3,4,16,128]{3,2,1,0:T(8,128)S(1)}, f32[3,4,16,128]{3,2,1,0:T(8,128)S(1)}, u32[]{:S(2)}, u32[]{:S(2)}) collective-permute-start(f32[3,4,16,128]{3,2,1,0:T(8,128)S(1)} %get-tuple-element.19), channel_id=1, source_target_pairs={{0,960},{64,0},{128,64},{192,128},{256,192},{320,256},{384,320},{4... | collective-permute-start | bytes 294920 | tf_op jit(solution)/shard_map/ppermute | solution.py:273
  59.0 7.0 %collective-permute-start.3 = (f32[16,4,128]{2,1,0:T(4,128)S(1)}, f32[16,4,128]{2,1,0:T(4,128)S(1)}, u32[]{:S(2)}, u32[]{:S(2)}) collective-permute-start(f32[16,4,128]{2,1,0:T(4,128)S(1)} %slice.4), channel_id=1, source_target_pairs={{0,16},{16,32},{32,48},{48,0},{8,56},{24,8},{40,24},{56,40},{1,17}... | collective-permute-start | bytes 98312 | tf_op jit(solution)/shard_map/ppermute | solution.py:286
